TPU v7x, 32 devices: a whole 2x2x4 slice. The times are simulated.
32 devices in a mesh: group: 2 (over core), fsdp: 4 (over z), tp: 4 (over y, x).
Axes of the slice: x: 2, y: 2, z: 4, core: 2. Of those that a mesh axis runs over, the one named last changes fastest.
Arguments:
- text_embeds: bfloat16 [4096, 8192], P(('group', 'fsdp'), 'tp'), may hold values from -6 to 6
- image_embeds: bfloat16 [2048, 8192], P(('group', 'fsdp'), 'tp'), may hold values from -6 to 6
- key_weight: bfloat16 [8192, 512], P(('group', 'fsdp')), may hold values from -0.0625 to 0.0625
- key_bias: float32 [512], P('tp'), may hold values from -3 to 3
- key_cot: bfloat16 [4096, 512], P(('group', 'fsdp')), may hold values from -6 to 6
- image_owner: int32 [2048], P(('group', 'fsdp')), may hold values from 0 to 7, as said below
- image_slot: int32 [4096], P(('group', 'fsdp')), may hold values from -1 to 511, as said below
- seq_lengths: int32 [16], P(('group', 'fsdp')), may hold values from 248 to 256, as said below
Outputs:
- key_rows: bfloat16 [4096, 512], P(('group', 'fsdp'), 'tp')
- text_grad: bfloat16 [4096, 8192], P(('group', 'fsdp'), 'tp')
- image_grad: bfloat16 [2048, 8192], P(('group', 'fsdp'), 'tp')
- weight_grad: float32 [8192, 512], P(('group', 'fsdp'), 'tp')
Inputs may be any that keep to these rules, and one draw needn't show every extreme that they name: `image_owner`: A source block of 256 image tokens sends at most 64 of them to one owner, and some block sends exactly 64 to some owner; an owner takes at most 448 image tokens in all, and some owner takes exactly that many. Every image token has exactly one position, as step one says. `image_slot`: slots are distinct within an owner block, and image tokens sit only at live positions. `seq_lengths`: some sequence has length 256.
All inputs are finite; a program needn't handle non-finite values.
Results may differ from a plain program's by a relative error of at most 0.0046.
Values may be sent and summed in bfloat16 or wider, within the bound.
A program may use at most 64 MiB of HBM per device.

v0:
```python
import jax
import jax.numpy as jnp
from jax import lax
from jax.experimental import pallas as pl
from jax.experimental.pallas import tpu as pltpu
from jax.sharding import PartitionSpec as P

HEAD_DIM = 128
LENGTH = 256


ROPE_BASE = 1000000.0


def angles(row_total):
    position = (jnp.arange(row_total, dtype=jnp.int32) % LENGTH).astype(jnp.float32)
    frequency = ROPE_BASE ** (-(jnp.arange(HEAD_DIM // 2, dtype=jnp.float32) * 2.0) / HEAD_DIM)
    angle_table = position[:, None] * frequency[None, :]
    return (jnp.cos(angle_table), jnp.sin(angle_table))


def rotate(values, cosine, sine, direction):
    row_total = values.shape[0]
    by_head = values.reshape(row_total, -1, HEAD_DIM)
    half_dim = HEAD_DIM // 2
    front_half = by_head[..., :half_dim]
    second = by_head[..., half_dim:]
    cos_part = cosine[:, None, :]
    sin_part = direction * sine[:, None, :]
    rotated = jnp.concatenate(
        [front_half * cos_part - second * sin_part, second * cos_part + front_half * sin_part],
        axis=-1,
    )
    return rotated.reshape(row_total, -1)


def send_slots(owners, unit_count, capacity):
    onehot_marks = (owners[:, None] == jnp.arange(unit_count, dtype=jnp.int32)[None, :]).astype(
        jnp.int32
    )
    before = jnp.cumsum(onehot_marks, axis=0) - onehot_marks
    owner_rank = jnp.sum(before * onehot_marks, axis=1)
    return owners * capacity + owner_rank


def share_kernel(text_ref, image_ref, back_ref, image_back_ref, out_ref):
    contract = (((0,), (0,)), ((), ()))
    part = lax.dot_general(
        text_ref[...], back_ref[...], contract, preferred_element_type=jnp.float32
    ) + lax.dot_general(
        image_ref[...], image_back_ref[...], contract, preferred_element_type=jnp.float32
    )
    part = part.astype(out_ref.dtype)
    width = out_ref.shape[2]
    for head in range(out_ref.shape[0]):
        out_ref[head] = part[:, head * width : (head + 1) * width]


def weight_shares(text, image, back, image_back, head_cols):
    columns = text.shape[1]
    heads = back.shape[1] // head_cols
    tile = min(512, columns)
    return pl.pallas_call(
        share_kernel,
        grid=(columns // tile,),
        in_specs=[
            pl.BlockSpec((text.shape[0], tile), lambda i: (0, i)),
            pl.BlockSpec((image.shape[0], tile), lambda i: (0, i)),
            pl.BlockSpec(back.shape, lambda i: (0, 0)),
            pl.BlockSpec(image_back.shape, lambda i: (0, 0)),
        ],
        out_specs=pl.BlockSpec((heads, tile, head_cols), lambda i: (0, i, 0)),
        out_shape=jax.ShapeDtypeStruct((heads, columns, head_cols), jnp.bfloat16),
        cost_estimate=pl.CostEstimate(
            flops=2 * (text.size + image.size) * back.shape[1],
            bytes_accessed=2 * (text.size + image.size + columns * back.shape[1]),
            transcendentals=0,
        ),
    )(text, image, back, image_back)


def project_kernel(text_ref, image_ref, weight_ref, out_ref):
    step = pl.program_id(0)
    last = pl.num_programs(0) - 1
    rows = jnp.where(step == last, image_ref[...], text_ref[...])
    part = jnp.dot(rows, weight_ref[...], preferred_element_type=jnp.float32).astype(out_ref.dtype)
    width = out_ref.shape[2]
    for head in range(out_ref.shape[0]):
        out_ref[head] = part[:, head * width : (head + 1) * width]


def projection_parts(text, image, weight, head_cols):
    heads = weight.shape[1] // head_cols
    tile, columns = image.shape
    text_tiles = text.shape[0] // tile
    return pl.pallas_call(
        project_kernel,
        grid=(text_tiles + 1,),
        in_specs=[
            pl.BlockSpec((tile, columns), lambda i: (jnp.minimum(i, text_tiles - 1), 0)),
            pl.BlockSpec((tile, columns), lambda i: (0, 0)),
            pl.BlockSpec(weight.shape, lambda i: (0, 0)),
        ],
        out_specs=pl.BlockSpec((heads, tile, head_cols), lambda i: (0, i, 0)),
        out_shape=jax.ShapeDtypeStruct((heads, text.shape[0] + tile, head_cols), jnp.bfloat16),
        cost_estimate=pl.CostEstimate(
            flops=2 * (text.size + image.size) * weight.shape[1],
            bytes_accessed=2 * (text.size + image.size + weight.size),
            transcendentals=0,
        ),
    )(text, image, weight)


def spread(piece, axis):
    count = lax.axis_size(axis)
    copies = jnp.broadcast_to(piece[None], (count,) + piece.shape)
    got = lax.all_to_all(copies, axis, split_axis=0, concat_axis=0, tiled=True)
    return got.reshape((count * piece.shape[0],) + piece.shape[1:])


def shifted(values, axis, step):
    count = lax.axis_size(axis)
    return lax.ppermute(values, axis, [(i, (i + step) % count) for i in range(count)])


def exchange_sum(blocks, axis):
    count = lax.axis_size(axis)
    me = lax.axis_index(axis)
    total = lax.dynamic_index_in_dim(blocks, me, 0, keepdims=False).astype(jnp.float32)
    for step in range(1, count):
        block = lax.dynamic_index_in_dim(blocks, (me + step) % count, 0, keepdims=False)
        total = total + shifted(block, axis, step).astype(jnp.float32)
    return total


def share_rows(piece, axis):
    count = lax.axis_size(axis)
    me = lax.axis_index(axis)
    rows = piece.shape[0]
    full = jnp.zeros((count * rows,) + piece.shape[1:], piece.dtype)
    full = lax.dynamic_update_slice_in_dim(full, piece, me * rows, 0)
    for step in range(1, count):
        source = (me + count - step) % count
        full = lax.dynamic_update_slice_in_dim(full, shifted(piece, axis, step), source * rows, 0)
    return full


def per_device(
    text_embeds, image_embeds, key_weight, key_bias, key_cot, image_owner, image_slot, seq_lengths
):
    row_count, columns = text_embeds.shape
    image_count = image_embeds.shape[0]
    units = ("group", "fsdp")
    core_count = lax.axis_size("group")
    fsdp_count = lax.axis_size("fsdp")
    tp_count = lax.axis_size("tp")
    unit_count = core_count * fsdp_count
    capacity = row_count // unit_count
    slot_count = unit_count * capacity
    head_cols = key_bias.shape[0]
    key_cols = head_cols * tp_count
    weight_block = key_weight.shape[0]
    halves = unit_count // tp_count
    tp_index = lax.axis_index("tp")

    position = jnp.arange(row_count, dtype=jnp.int32)
    seq_ids = position // LENGTH
    seq_marks = seq_ids[:, None] == jnp.arange(seq_lengths.shape[0], dtype=jnp.int32)[None, :]
    live_limit = jnp.sum(jnp.where(seq_marks, seq_lengths[None, :], 0), axis=1)
    live_mask = (position % LENGTH < live_limit).astype(jnp.float32)
    cosine, sine = angles(row_count)
    masked = key_cot.astype(jnp.float32) * live_mask[:, None]
    rotated_back = rotate(masked, cosine, sine, -1.0).astype(jnp.bfloat16)
    is_image = image_slot >= 0
    text_back = jnp.where(is_image[:, None], jnp.zeros_like(rotated_back), rotated_back)

    slot_ids = jnp.arange(slot_count, dtype=jnp.int32)
    place = (image_slot[:, None] == slot_ids[None, :]).astype(jnp.bfloat16)
    returning = lax.dot_general(
        place, rotated_back, (((0,), (0,)), ((), ())), preferred_element_type=jnp.float32
    ).astype(jnp.bfloat16)
    returned = lax.all_to_all(
        returning.reshape(unit_count, capacity, key_cols), units, split_axis=0, concat_axis=0,
        tiled=True,
    ).reshape(slot_count, key_cols)
    slots_out = send_slots(image_owner, unit_count, capacity)
    pick = (slots_out[:, None] == slot_ids[None, :]).astype(jnp.bfloat16)
    image_back = jnp.dot(pick, returned, preferred_element_type=jnp.float32).astype(jnp.bfloat16)

    piece_rows = weight_block // tp_count
    own_piece = lax.dynamic_slice_in_dim(key_weight, tp_index * piece_rows, piece_rows, 0)
    moves = []
    for unit in range(unit_count):
        for part in range(tp_count):
            target = (unit % halves) * tp_count + part
            moves.append((unit * tp_count + part, target * tp_count + unit // halves))
    own_piece = lax.ppermute(own_piece, units + ("tp",), moves)
    chip_rows = spread(own_piece, "fsdp")

    shares = weight_shares(text_embeds, image_embeds, text_back, image_back, head_cols)
    shares = shares.reshape(core_count, fsdp_count, weight_block, head_cols)
    shares = exchange_sum(shares, "group").astype(jnp.bfloat16)
    shares, chip_rows = lax.optimization_barrier((shares, chip_rows))
    shares = lax.all_to_all(shares, "fsdp", split_axis=0, concat_axis=0, tiled=True)
    weight_grad = jnp.sum(shares.astype(jnp.float32), axis=0) / row_count
    returns = []
    for unit in range(unit_count):
        for part in range(tp_count):
            holder = (unit % halves) + part * halves
            returns.append((holder * tp_count + unit // halves, unit * tp_count + part))
    weight_grad = lax.ppermute(weight_grad, units + ("tp",), returns)

    weight_rows = share_rows(chip_rows, "group")
    both = projection_parts(text_embeds, image_embeds, weight_rows, head_cols)
    both = exchange_sum(both, "tp")
    image_proj = both[row_count:].astype(jnp.bfloat16)
    outgoing = lax.dot_general(
        pick, image_proj, (((0,), (0,)), ((), ())), preferred_element_type=jnp.float32
    ).astype(jnp.bfloat16)
    received = lax.all_to_all(
        outgoing.reshape(unit_count, capacity, head_cols), units, split_axis=0, concat_axis=0,
        tiled=True,
    ).reshape(slot_count, head_cols)
    placed = jnp.dot(place, received, preferred_element_type=jnp.float32)
    projected = jnp.where(is_image[:, None], placed, both[:row_count]) + key_bias
    key_rows = (rotate(projected, cosine, sine, 1.0) * live_mask[:, None]).astype(jnp.bfloat16)

    contract = (((1,), (1,)), ((), ()))
    text_grad = lax.dot_general(
        text_back, weight_rows, contract, preferred_element_type=jnp.float32
    ).astype(jnp.bfloat16)
    image_grad = lax.dot_general(
        image_back, weight_rows, contract, preferred_element_type=jnp.float32
    ).astype(jnp.bfloat16)
    return (key_rows, text_grad, image_grad, weight_grad)


def solution(mesh):
    in_specs = (
        P(("group", "fsdp"), "tp"),
        P(("group", "fsdp"), "tp"),
        P(("group", "fsdp"), None),
        P("tp"),
        P(("group", "fsdp"), None),
        P(("group", "fsdp")),
        P(("group", "fsdp")),
        P(("group", "fsdp")),
    )
    out_specs = (
        P(("group", "fsdp"), "tp"),
        P(("group", "fsdp"), "tp"),
        P(("group", "fsdp"), "tp"),
        P(("group", "fsdp"), "tp"),
    )
    return jax.shard_map(
        per_device, mesh=mesh, in_specs=in_specs, out_specs=out_specs, check_vma=False
    )
```

profile of v0, /device:TPU:3, one launch (start us, length us, event | category | flops | bytes accessed | tf_op | source)
XLA Modules:
  0.0 136.4 jit_solution(12772641685637158837)
XLA Ops:
  0.7 0.8 fusion.24
  1.5 1.2 convert_multiply_fusion
  2.7 0.4 reshape.211
  3.1 1.0 multiply_cosine_fusion.1
  4.1 0.9 subtract_convert_fusion
  4.9 0.7 pad_maximum_fusion
  5.7 1.4 convolution_convert_fusion.2
  7.0 5.6 %all-to-all-start = ((bf16[8,64,512]{2,1,0:T(8,128)(2,1)}), bf16[8,64,512]{2,1,0:T(8,128)(2,1)S(1)}, u32[]{:S(2)}, u32[]{:S(2)}) async-start(bf16[8,64,512]{2,1,0:T(8,128)(2,1)} %bitcast.3), calls=%async_computation | async-start | bytes 1048576 | tf_op jit(solution)/shard_map/all_to_all | solution.py:182
  12.6 4.5 %collective-permute-start.1 = (bf16[256,512]{1,0:T(8,128)(2,1)S(1)}, bf16[256,512]{1,0:T(8,128)(2,1)S(1)}, u32[]{:S(2)}, u32[]{:S(2)}) collective-permute-start(bf16[256,512]{1,0:T(8,128)(2,1)S(1)} %constant_dynamic-slice_fusion), channel_id=1, source_target_pairs={{0,0},{1,4},{2,8},{3,12},{4,16},{5,20},{6,24},{7,28},{8,1},{9,5},{... | collective-permute-start | bytes 786440 | tf_op jit(solution)/shard_map/ppermute | solution.py:197
  17.1 0.6 reduce-window.6
  17.7 0.2 slice_reduce_fusion
  18.1 0.9 bitcast_select_fusion.back_ref
  19.0 12.1 %collective-permute-done.1 = bf16[256,512]{1,0:T(8,128)(2,1)S(1)} collective-permute-done((bf16[256,512]{1,0:T(8,128)(2,1)S(1)}, bf16[256,512]{1,0:T(8,128)(2,1)S(1)}, u32[]{:S(2)}, u32[]{:S(2)}) %collective-permute-start.1) | collective-permute-done | bytes 262176 | tf_op jit(solution)/shard_map/ppermute | solution.py:197
  31.1 2.3 %all-to-all-done = bf16[8,64,512]{2,1,0:T(8,128)(2,1)S(1)} async-done(((bf16[8,64,512]{2,1,0:T(8,128)(2,1)}), bf16[8,64,512]{2,1,0:T(8,128)(2,1)S(1)}, u32[]{:S(2)}, u32[]{:S(2)}) %all-to-all-start) | async-done | bytes 524320 | tf_op jit(solution)/shard_map/all_to_all | solution.py:182
  33.4 1.1 broadcast_in_dim.37
  34.5 5.3 %all-to-all-start.1 = ((bf16[4,256,512]{2,1,0:T(8,128)(2,1)}), bf16[4,256,512]{2,1,0:T(8,128)(2,1)}, u32[]{:S(2)}, u32[]{:S(2)}) async-start(bf16[4,256,512]{2,1,0:T(8,128)(2,1)} %broadcast_in_dim.37), calls=%async_computation.1 | async-start | bytes 2097152 | tf_op jit(solution)/shard_map/all_to_all | solution.py:117
  39.8 1.1 convolution_convert_fusion.3.image_back_ref
  40.8 5.4 %shard_map.111 = bf16[4,2048,128]{2,1,0:T(8,128)(2,1)} custom-call(bf16[512,2048]{1,0:T(8,128)(2,1)} %text_ref.3, bf16[256,2048]{1,0:T(8,128)(2,1)} %image_ref.3, bf16[512,512]{1,0:T(8,128)(2,1)} %bitcast_select_fusion.back_ref, bf16[256,512]{1,0:T(8,128)(2,1)} %convolution_convert_fusion.3.image_back_ref), custom_call_target="tpu_custom_call" | custom-call | flops 1610612736 | bytes 5242880 | tf_op jit(solution)/shard_map/pallas_call | solution.py:63
  46.2 2.4 %dynamic-slice_bitcast_fusion = bf16[4,1024,128]{2,1,0:T(8,128)(2,1)} fusion(bf16[2,4,1024,128]{3,2,1,0:T(8,128)(2,1)} %bitcast.48, s32[]{:T(128)S(6)} %select_n.108), kind=kLoop, calls=%fused_computation.8 | loop fusion | bytes 2097156 | tf_op jit(solution)/shard_map/jit(dynamic_index_in_dim)/squeeze | solution.py:131
  48.6 6.8 %collective-permute-start = (bf16[4,1024,128]{2,1,0:T(8,128)(2,1)}, bf16[4,1024,128]{2,1,0:T(8,128)(2,1)}, u32[]{:S(2)}, u32[]{:S(2)}) collective-permute-start(bf16[4,1024,128]{2,1,0:T(8,128)(2,1)} %dynamic-slice_bitcast_fusion), channel_id=1, source_target_pairs={{0,16},{16,0},{1,17},{17,1},{2,18},{18,2},{3,19},{19,3},{4,20},{20... | collective-permute-start | bytes 3145736 | tf_op jit(solution)/shard_map/ppermute | solution.py:123
  55.4 2.6 %collective-permute-done = bf16[4,1024,128]{2,1,0:T(8,128)(2,1)} collective-permute-done((bf16[4,1024,128]{2,1,0:T(8,128)(2,1)}, bf16[4,1024,128]{2,1,0:T(8,128)(2,1)}, u32[]{:S(2)}, u32[]{:S(2)}) %collective-permute-start) | collective-permute-done | bytes 1048608 | tf_op jit(solution)/shard_map/ppermute | solution.py:123
  58.0 2.5 %fusion = bf16[4,1024,128]{2,1,0:T(8,128)(2,1)} fusion(bf16[4,1024,128]{2,1,0:T(8,128)(2,1)} %collective-permute-done, bf16[2,4,1024,128]{3,2,1,0:T(8,128)(2,1)S(1)} %bitcast.49, s32[]{:T(128)S(6)} %select_n.106), kind=kLoop, calls=%fused_computation.3 | loop fusion | flops 2097152 | bytes 3145732 | tf_op jit(solution)/shard_map/convert_element_type | solution.py:202
  60.5 2.7 %all-to-all-done.1 = bf16[4,256,512]{2,1,0:T(8,128)(2,1)} async-done(((bf16[4,256,512]{2,1,0:T(8,128)(2,1)}), bf16[4,256,512]{2,1,0:T(8,128)(2,1)}, u32[]{:S(2)}, u32[]{:S(2)}) %all-to-all-start.1) | async-done | bytes 1048608 | tf_op jit(solution)/shard_map/all_to_all | solution.py:117
  63.2 4.0 %collective-permute-start.2 = (bf16[1024,512]{1,0:T(8,128)(2,1)}, bf16[1024,512]{1,0:T(8,128)(2,1)}, u32[]{:S(2)}, u32[]{:S(2)}) collective-permute-start(bf16[1024,512]{1,0:T(8,128)(2,1)} %bitcast.8), channel_id=1, source_target_pairs={{0,16},{16,0},{1,17},{17,1},{2,18},{18,2},{3,19},{19,3},{4,20},{20... | collective-permute-start | bytes 3145736 | tf_op jit(solution)/shard_map/ppermute | solution.py:123
  67.1 4.2 %all-to-all-start.3 = ((bf16[4,1024,128]{2,1,0:T(8,128)(2,1)}), bf16[4,1024,128]{2,1,0:T(8,128)(2,1)}, u32[]{:S(2)}, u32[]{:S(2)}) async-start(bf16[4,1024,128]{2,1,0:T(8,128)(2,1)} %fusion), calls=%async_computation.3 | async-start | bytes 2097152 | tf_op jit(solution)/shard_map/all_to_all | solution.py:204
  71.5 1.3 constant_dynamic-update-slice_fusion.1
  72.9 1.3 constant_dynamic-update-slice_fusion.weight_ref
  74.2 1.3 copy-done.1
  75.6 5.1 %shard_map.112 = bf16[4,768,128]{2,1,0:T(8,128)(2,1)} custom-call(bf16[512,2048]{1,0:T(8,128)(2,1)} %text_ref.3, bf16[256,2048]{1,0:T(8,128)(2,1)} %image_ref.3, bf16[2048,512]{1,0:T(8,128)(2,1)} %copy-done.1), custom_call_target="tpu_custom_call" | custom-call | flops 1610612736 | bytes 5242880 | tf_op jit(solution)/shard_map/pallas_call | solution.py:96
  80.7 1.2 dynamic-slice_bitcast_fusion.3
  81.9 0.7 collective-permute-start.3
  82.6 3.8 %collective-permute-start.4 = (bf16[768,128]{1,0:T(8,128)(2,1)S(1)}, bf16[768,128]{1,0:T(8,128)(2,1)S(1)}, u32[]{:S(2)}, u32[]{:S(2)}) collective-permute-start(bf16[768,128]{1,0:T(8,128)(2,1)S(1)} %get-tuple-element.12), channel_id=1, source_target_pairs={{0,2},{1,3},{2,0},{3,1},{4,6},{5,7},{6,4},{7,5},{8,10},{9,11},{10,... | collective-permute-start | bytes 589832 | tf_op jit(solution)/shard_map/ppermute | solution.py:123
  86.4 1.4 %collective-permute-start.5 = (bf16[768,128]{1,0:T(8,128)(2,1)S(1)}, bf16[768,128]{1,0:T(8,128)(2,1)S(1)}, u32[]{:S(2)}, u32[]{:S(2)}) collective-permute-start(bf16[768,128]{1,0:T(8,128)(2,1)S(1)} %get-tuple-element.11), channel_id=1, source_target_pairs={{0,3},{1,0},{2,1},{3,2},{4,7},{5,4},{6,5},{7,6},{8,11},{9,8},{10,9... | collective-permute-start | bytes 589832 | tf_op jit(solution)/shard_map/ppermute | solution.py:123
  87.8 4.4 %convolution_convert_fusion = bf16[512,2048]{1,0:T(8,128)(2,1)} fusion(bf16[512,512]{1,0:T(8,128)(2,1)} %bitcast_select_fusion.back_ref, bf16[2048,512]{1,0:T(8,128)(2,1)} %copy-done.1), kind=kOutput, calls=%fused_computation | convolution fusion | flops 1074790400 | bytes 4718592 | tf_op jit(solution)/shard_map/dot_general | solution.py:229
  92.2 1.7 %convolution_convert_fusion.1 = bf16[256,2048]{1,0:T(8,128)(2,1)} fusion(bf16[256,512]{1,0:T(8,128)(2,1)S(1)} %copy-done.4, bf16[2048,512]{1,0:T(8,128)(2,1)S(1)} %copy-done.2), kind=kOutput, calls=%fused_computation.1 | convolution fusion | flops 537395200 | bytes 3407872 | tf_op jit(solution)/shard_map/dot_general | solution.py:232
  93.9 0.9 collective-permute-done.4
  94.7 2.1 %collective-permute-done.5 = bf16[768,128]{1,0:T(8,128)(2,1)S(1)} collective-permute-done((bf16[768,128]{1,0:T(8,128)(2,1)S(1)}, bf16[768,128]{1,0:T(8,128)(2,1)S(1)}, u32[]{:S(2)}, u32[]{:S(2)}) %collective-permute-start.5) | collective-permute-done | bytes 196640 | tf_op jit(solution)/shard_map/ppermute | solution.py:123
  96.8 1.0 fusion.7
  97.8 1.1 convolution_convert_fusion.4
  98.9 5.5 %all-to-all-start.2 = ((bf16[8,64,128]{2,1,0:T(8,128)(2,1)}), bf16[8,64,128]{2,1,0:T(8,128)(2,1)S(1)}, u32[]{:S(2)}, u32[]{:S(2)}) async-start(bf16[8,64,128]{2,1,0:T(8,128)(2,1)} %bitcast.13), calls=%async_computation.2 | async-start | bytes 262144 | tf_op jit(solution)/shard_map/all_to_all | solution.py:220
  104.4 1.4 %convert_reduce_fusion = f32[1024,128]{1,0:T(8,128)S(1)} fusion(bf16[4,1024,128]{2,1,0:T(8,128)(2,1)} %all-to-all-done.3), kind=kLoop, calls=%fused_computation.4 | loop fusion | flops 917504 | bytes 1572864 | tf_op jit(solution)/shard_map/reduce_sum | solution.py:205
  105.9 4.2 %collective-permute-start.6 = (f32[1024,128]{1,0:T(8,128)S(1)}, f32[1024,128]{1,0:T(8,128)S(1)}, u32[]{:S(2)}, u32[]{:S(2)}) collective-permute-start(f32[1024,128]{1,0:T(8,128)S(1)} %broadcast_multiply_fusion), channel_id=1, source_target_pairs={{0,0},{8,1},{16,2},{24,3},{4,4},{12,5},{20,6},{28,7},{1,8},{9,9},{... | collective-permute-start | bytes 1572872 | tf_op jit(solution)/shard_map/ppermute | solution.py:211
  110.1 0.9 all-to-all-done.2
  111.0 0.4 fusion.16
  111.3 1.2 fusion.12
  112.5 0.9 fusion.18
  113.4 22.2 %collective-permute-done.6 = f32[1024,128]{1,0:T(8,128)S(1)} collective-permute-done((f32[1024,128]{1,0:T(8,128)S(1)}, f32[1024,128]{1,0:T(8,128)S(1)}, u32[]{:S(2)}, u32[]{:S(2)}) %collective-permute-start.6) | collective-permute-done | bytes 524320 | tf_op jit(solution)/shard_map/ppermute | solution.py:211
  135.6 0.8 copy.25
  (30 shorter events, 0.4 us)
Async XLA Ops:
  0.6 12.0 %copy-start = (bf16[1024,512]{1,0:T(8,128)(2,1)S(1)}, bf16[1024,512]{1,0:T(8,128)(2,1)}, u32[]{:S(2)}) copy-start(bf16[1024,512]{1,0:T(8,128)(2,1)} %param.10) | copy-start | bytes 3145732
  4.0 1.6 %copy-start.6 = (s32[512]{0:T(512)S(1)}, s32[512]{0:T(512)}, u32[]{:S(2)}) copy-start(s32[512]{0:T(512)} %param.14) | copy-start | bytes 6148
  4.9 12.2 %copy-start.5 = (s32[256]{0:T(256)S(1)}, s32[256]{0:T(256)}, u32[]{:S(2)}) copy-start(s32[256]{0:T(256)} %param.13) | copy-start | bytes 3076
  7.0 26.4 %all-to-all-start = ((bf16[8,64,512]{2,1,0:T(8,128)(2,1)}), bf16[8,64,512]{2,1,0:T(8,128)(2,1)S(1)}, u32[]{:S(2)}, u32[]{:S(2)}) async-start(bf16[8,64,512]{2,1,0:T(8,128)(2,1)} %bitcast.3), calls=%async_computation | async-start | bytes 1048576 | tf_op jit(solution)/shard_map/all_to_all | solution.py:182
  12.6 18.5 %collective-permute-start.1 = (bf16[256,512]{1,0:T(8,128)(2,1)S(1)}, bf16[256,512]{1,0:T(8,128)(2,1)S(1)}, u32[]{:S(2)}, u32[]{:S(2)}) collective-permute-start(bf16[256,512]{1,0:T(8,128)(2,1)S(1)} %constant_dynamic-slice_fusion), channel_id=1, source_target_pairs={{0,0},{1,4},{2,8},{3,12},{4,16},{5,20},{6,24},{7,28},{8,1},{9,5},{... | collective-permute-start | bytes 786440 | tf_op jit(solution)/shard_map/ppermute | solution.py:197
  34.5 28.7 %all-to-all-start.1 = ((bf16[4,256,512]{2,1,0:T(8,128)(2,1)}), bf16[4,256,512]{2,1,0:T(8,128)(2,1)}, u32[]{:S(2)}, u32[]{:S(2)}) async-start(bf16[4,256,512]{2,1,0:T(8,128)(2,1)} %broadcast_in_dim.37), calls=%async_computation.1 | async-start | bytes 2097152 | tf_op jit(solution)/shard_map/all_to_all | solution.py:117
  46.2 11.8 %copy-start.3 = (bf16[4,2048,128]{2,1,0:T(8,128)(2,1)S(1)}, bf16[4,2048,128]{2,1,0:T(8,128)(2,1)}, u32[]{:S(2)}) copy-start(bf16[4,2048,128]{2,1,0:T(8,128)(2,1)} %shard_map.111) | copy-start | bytes 6291460
  48.6 9.4 %collective-permute-start = (bf16[4,1024,128]{2,1,0:T(8,128)(2,1)}, bf16[4,1024,128]{2,1,0:T(8,128)(2,1)}, u32[]{:S(2)}, u32[]{:S(2)}) collective-permute-start(bf16[4,1024,128]{2,1,0:T(8,128)(2,1)} %dynamic-slice_bitcast_fusion), channel_id=1, source_target_pairs={{0,16},{16,0},{1,17},{17,1},{2,18},{18,2},{3,19},{19,3},{4,20},{20... | collective-permute-start | bytes 3145736 | tf_op jit(solution)/shard_map/ppermute | solution.py:123
  63.2 9.7 %collective-permute-start.2 = (bf16[1024,512]{1,0:T(8,128)(2,1)}, bf16[1024,512]{1,0:T(8,128)(2,1)}, u32[]{:S(2)}, u32[]{:S(2)}) collective-permute-start(bf16[1024,512]{1,0:T(8,128)(2,1)} %bitcast.8), channel_id=1, source_target_pairs={{0,16},{16,0},{1,17},{17,1},{2,18},{18,2},{3,19},{19,3},{4,20},{20... | collective-permute-start | bytes 3145736 | tf_op jit(solution)/shard_map/ppermute | solution.py:123
  67.1 31.8 %all-to-all-start.3 = ((bf16[4,1024,128]{2,1,0:T(8,128)(2,1)}), bf16[4,1024,128]{2,1,0:T(8,128)(2,1)}, u32[]{:S(2)}, u32[]{:S(2)}) async-start(bf16[4,1024,128]{2,1,0:T(8,128)(2,1)} %fusion), calls=%async_computation.3 | async-start | bytes 2097152 | tf_op jit(solution)/shard_map/all_to_all | solution.py:204
  74.2 1.3 copy-start.1
  81.9 12.0 %collective-permute-start.3 = (bf16[768,128]{1,0:T(8,128)(2,1)S(1)}, bf16[768,128]{1,0:T(8,128)(2,1)S(1)}, u32[]{:S(2)}, u32[]{:S(2)}) collective-permute-start(bf16[768,128]{1,0:T(8,128)(2,1)S(1)} %get-tuple-element.10), channel_id=1, source_target_pairs={{0,1},{1,2},{2,3},{3,0},{4,5},{5,6},{6,7},{7,4},{8,9},{9,10},{10,1... | collective-permute-start | bytes 589832 | tf_op jit(solution)/shard_map/ppermute | solution.py:123
  82.6 12.2 %collective-permute-start.4 = (bf16[768,128]{1,0:T(8,128)(2,1)S(1)}, bf16[768,128]{1,0:T(8,128)(2,1)S(1)}, u32[]{:S(2)}, u32[]{:S(2)}) collective-permute-start(bf16[768,128]{1,0:T(8,128)(2,1)S(1)} %get-tuple-element.12), channel_id=1, source_target_pairs={{0,2},{1,3},{2,0},{3,1},{4,6},{5,7},{6,4},{7,5},{8,10},{9,11},{10,... | collective-permute-start | bytes 589832 | tf_op jit(solution)/shard_map/ppermute | solution.py:123
  86.4 5.8 %copy-start.2 = (bf16[2048,512]{1,0:T(8,128)(2,1)S(1)}, bf16[2048,512]{1,0:T(8,128)(2,1)}, u32[]{:S(2)}) copy-start(bf16[2048,512]{1,0:T(8,128)(2,1)} %copy-done.1) | copy-start | bytes 6291460
  86.4 5.8 %copy-start.4 = (bf16[256,512]{1,0:T(8,128)(2,1)S(1)}, bf16[256,512]{1,0:T(8,128)(2,1)}, u32[]{:S(2)}) copy-start(bf16[256,512]{1,0:T(8,128)(2,1)} %convolution_convert_fusion.3.image_back_ref) | copy-start | bytes 786436
  86.4 10.4 %collective-permute-start.5 = (bf16[768,128]{1,0:T(8,128)(2,1)S(1)}, bf16[768,128]{1,0:T(8,128)(2,1)S(1)}, u32[]{:S(2)}, u32[]{:S(2)}) collective-permute-start(bf16[768,128]{1,0:T(8,128)(2,1)S(1)} %get-tuple-element.11), channel_id=1, source_target_pairs={{0,3},{1,0},{2,1},{3,2},{4,7},{5,4},{6,5},{7,6},{8,11},{9,8},{10,9... | collective-permute-start | bytes 589832 | tf_op jit(solution)/shard_map/ppermute | solution.py:123
  93.9 17.1 %copy-start.7 = (f32[128]{0:T(128)S(1)}, f32[128]{0:T(128)}, u32[]{:S(2)}) copy-start(f32[128]{0:T(128)} %param.11) | copy-start | bytes 1540
  98.9 12.1 %all-to-all-start.2 = ((bf16[8,64,128]{2,1,0:T(8,128)(2,1)}), bf16[8,64,128]{2,1,0:T(8,128)(2,1)S(1)}, u32[]{:S(2)}, u32[]{:S(2)}) async-start(bf16[8,64,128]{2,1,0:T(8,128)(2,1)} %bitcast.13), calls=%async_computation.2 | async-start | bytes 262144 | tf_op jit(solution)/shard_map/all_to_all | solution.py:220
  105.9 29.7 %collective-permute-start.6 = (f32[1024,128]{1,0:T(8,128)S(1)}, f32[1024,128]{1,0:T(8,128)S(1)}, u32[]{:S(2)}, u32[]{:S(2)}) collective-permute-start(f32[1024,128]{1,0:T(8,128)S(1)} %broadcast_multiply_fusion), channel_id=1, source_target_pairs={{0,0},{8,1},{16,2},{24,3},{4,4},{12,5},{20,6},{28,7},{1,8},{9,9},{... | collective-permute-start | bytes 1572872 | tf_op jit(solution)/shard_map/ppermute | solution.py:211
where the time goes:
time: 137 us; the launch traced here: 136 us
  starting transfers between devices  45.9 us (34%)
  waiting for transfers between devices  45.7 us (33%)
  other arithmetic  13.3 us (10%)
  Pallas kernels  10.5 us (8%)
  local copies, waits for them, and re-layouts  10.2 us (7%)
  matrix products  9.93 us (7%)
    ppermute x1, waiting for transfers between devices, per_device(): weight_grad = lax.ppermute(weight_grad, units + ('tp',), returns)  22.2 us
    ppermute x5, starting transfers between devices, shifted(): lax.ppermute(values, axis, [(i, (i + step) % count) for i in range(count)])  16.6 us
    ppermute x1, waiting for transfers between devices, per_device(): own_piece = lax.ppermute(own_piece, units + ('tp',), moves)  12.1 us
    ppermute x5, waiting for transfers between devices, shifted(): lax.ppermute(values, axis, [(i, (i + step) % count) for i in range(count)])  5.56 us
    all_to_all x1, starting transfers between devices, per_device(): lax.all_to_all(returning.reshape(unit_count, capacity, key_cols), units,...  5.55 us
    all_to_all x1, starting transfers between devices, per_device(): lax.all_to_all(outgoing.reshape(unit_count, capacity, head_cols), units,...  5.52 us
    pallas_call x1, Pallas kernels, weight_shares(): pl.pallas_call(share_kernel, grid=(columns // tile,), in_specs=[pl.BlockS...  5.36 us
    all_to_all x1, starting transfers between devices, spread(): got = lax.all_to_all(copies, axis, split_axis=0, concat_axis=0, tiled=True)  5.3 us
  transfers between devices with their start and end apart: 11, of which 8 were waited for; matrix products, arithmetic and copies ran while one was open for 18% of the time, Pallas kernels for 8%

commit v1 on v0

--- a/solution.py
+++ b/solution.py
@@ -1,5 +1,8 @@
+import functools
+
 import jax
 import jax.numpy as jnp
+import numpy as np
 from jax import lax
 from jax.experimental import pallas as pl
 from jax.experimental.pallas import tpu as pltpu
@@ -145,7 +148,7 @@
     return full
 
 
-def per_device(
+def per_device_plain(
     text_embeds, image_embeds, key_weight, key_bias, key_cot, image_owner, image_slot, seq_lengths
 ):
     row_count, columns = text_embeds.shape
@@ -235,6 +238,517 @@
     return (key_rows, text_grad, image_grad, weight_grad)
 
 
+MESH = pl.DeviceIdType.MESH
+HALF = HEAD_DIM // 2
+ROWS_TO_COLS = (((0,), (0,)), ((), ()))
+COLS_TO_COLS = (((1,), (1,)), ((), ()))
+W_PARTS = 4
+G_PARTS = 8
+
+
+def fused_kernel(
+    groups, fsdp, tp, capacity,
+    text_ref, image_ref, weight_ref, bias_ref, cot_ref, owner_ref, slot_ref, lens_ref, cos_ref, sin_ref,
+    keys_out, text_out, image_out, wgrad_out,
+    x, w, cot, cosv, sinv, back, pick_t, place_t, is_img,
+    d1_src, d1_dst, d2_src, pf, pa, pb, chain, above, below, y, yb, yr, c2_src, c2_dst, gout, landed, wg, keys,
+    ld, w_recv, w_up, w_dn, w_dd, d1_s, d1_r, d2_s, d2_r, ci_s, ci_r, ct_s, ct_r, c2_s, c2_r,
+    p_s, p_r, ab_r, be_r, ch_s, g_s, g_r, st,
+):
+    f32, bf16 = jnp.float32, jnp.bfloat16
+    g, z, t = lax.axis_index("group"), lax.axis_index("fsdp"), lax.axis_index("tp")
+    units = groups * fsdp
+    me = g * fsdp + z
+    rows, images = text_ref.shape[0], image_ref.shape[0]
+    both = rows + images
+    columns = text_ref.shape[1]
+    slots = units * capacity
+    cols = bias_ref.shape[1]
+    block = weight_ref.shape[0]
+    blocks = units // tp
+    w_rows, g_rows = block // W_PARTS, block // G_PARTS
+    w_steps, g_steps = blocks * W_PARTS, blocks * G_PARTS
+    first = t * blocks
+    carrier, z0 = first // fsdp, lax.rem(first, fsdp)
+    carries = g == carrier
+    inside = (z >= z0) & (z < z0 + blocks)
+    far_end = jnp.logical_not(inside) & ((z == 0) | (z == fsdp - 1))
+    adjacent = inside | (z == z0 - 1) | (z == z0 + blocks)
+    my_cols = pl.ds(pl.multiple_of(t * cols, cols), cols)
+    peer = (1 - g, z, t)
+
+    def near_block(k):
+        within = lax.rem(z - z0 + k + blocks, blocks)
+        return jnp.where(inside, within, jnp.where(z < z0, k, blocks - 1 - k))
+
+    def unit_of(i):
+        v = lax.rem(me + i, units)
+        return v, (v // fsdp, lax.rem(v, fsdp), t)
+
+    def head_of(i):
+        q = lax.rem(t + i, tp)
+        return q, (g, z, q)
+
+    def remote(src, dst, send, recv, device):
+        return pltpu.make_async_remote_copy(
+            src_ref=src, dst_ref=dst, send_sem=send, recv_sem=recv, device_id=device, device_id_type=MESH
+        )
+
+    barrier = pltpu.get_barrier_semaphore()
+    for i in range(1, units):
+        pl.semaphore_signal(barrier, inc=1, device_id=unit_of(i)[1], device_id_type=MESH)
+    for i in range(1, tp):
+        q = head_of(i)[0]
+        for core in range(groups):
+            pl.semaphore_signal(barrier, inc=1, device_id=(core, z, q), device_id_type=MESH)
+
+    loads = [
+        pltpu.make_async_copy(cot_ref, cot, ld.at[0]),
+        pltpu.make_async_copy(cos_ref, cosv, ld.at[1]),
+        pltpu.make_async_copy(sin_ref, sinv, ld.at[2]),
+        pltpu.make_async_copy(text_ref, x.at[pl.ds(0, rows)], ld.at[3]),
+        pltpu.make_async_copy(image_ref, x.at[pl.ds(rows, images)], ld.at[4]),
+    ]
+    for load in loads[:3]:
+        load.start()
+
+    def w_slice(b, c):
+        return pl.ds(pl.multiple_of(b * block + c * w_rows, w_rows), w_rows)
+
+    def w_load(b, c):
+        return pltpu.make_async_copy(
+            weight_ref.at[pl.ds(pl.multiple_of(c * w_rows, w_rows), w_rows)], w.at[w_slice(b, c)], w_recv.at[b * W_PARTS + c]
+        )
+
+    @pl.when(carries & inside)
+    def _():
+        for c in range(W_PARTS):
+            w_load(z - z0, c).start()
+
+    for load in loads[3:]:
+        load.start()
+
+    slot_ids = lax.broadcasted_iota(jnp.int32, (slots, rows), 0)
+    place_t[...] = jnp.where(slot_ids == slot_ref[...], 1.0, 0.0).astype(bf16)
+    is_img[...] = lax.dot_general(
+        place_t[...], jnp.ones((slots, cols), bf16), ROWS_TO_COLS, preferred_element_type=f32
+    )
+    row_ids = lax.broadcasted_iota(jnp.int32, (LENGTH, HEAD_DIM), 0)
+
+    def live(s):
+        return row_ids < lens_ref[0:1, s : s + 1]
+
+    def rotated_back(s, at):
+        span = pl.ds(s * LENGTH, LENGTH)
+        values = jnp.where(live(s), cot[span, at].astype(f32), 0.0)
+        return values * cosv[...] - pltpu.roll(values, HALF, 1) * sinv[...]
+
+    for load in loads[:3]:
+        load.wait()
+    mine = jnp.concatenate([rotated_back(s, my_cols) for s in range(rows // LENGTH)], axis=0).astype(bf16)
+    d1_src[...] = jnp.dot(place_t[...], mine, preferred_element_type=f32).astype(bf16)
+
+    pl.semaphore_wait(barrier, units - 1 + groups * (tp - 1))
+
+    def slot_rows(v):
+        return pl.ds(pl.multiple_of(v * capacity, capacity), capacity)
+
+    def d1(i):
+        v, device = unit_of(i)
+        return remote(d1_src.at[slot_rows(v)], d1_dst.at[slot_rows(me)], d1_s.at[v], d1_r.at[me], device)
+
+    for i in range(1, units):
+        d1(i).start()
+    d1_dst[slot_rows(me), :] = d1_src[slot_rows(me), :]
+
+    def w_send(b, c, to, sem):
+        i = b * W_PARTS + c
+        return remote(w.at[w_slice(b, c)], w.at[w_slice(b, c)], sem.at[i], w_recv.at[i], to)
+
+    def w_routes(b, c):
+        return (
+            ((z >= z0 + b) & (z < fsdp - 1), w_send(b, c, (g, z + 1, t), w_up)),
+            ((z <= z0 + b) & (z > 0), w_send(b, c, (g, z - 1, t), w_dn)),
+        )
+
+    def w_forward(n):
+        b, c = near_block(n // W_PARTS), lax.rem(n, W_PARTS)
+        w_load(b, c).wait()
+        for condition, copy in w_routes(b, c):
+            pl.when(condition)(copy.start)
+        w_send(b, c, peer, w_dd).start()
+
+    @pl.when(carries & inside)
+    def _():
+        lax.fori_loop(0, W_PARTS, lambda n, carry: (w_forward(n), carry)[1], 0)
+
+    base = jnp.where(inside, W_PARTS, 0)
+    early = 2
+
+    y[...] = jnp.zeros_like(y)
+    for s in range(rows // LENGTH):
+        span = pl.ds(s * LENGTH, LENGTH)
+        for h in range(tp):
+            at = pl.ds(h * cols, cols)
+            back[span, at] = jnp.where(is_img[span, :] > 0.5, 0.0, rotated_back(s, at)).astype(bf16)
+    image_units = lax.broadcasted_iota(jnp.int32, (units, images), 0)
+    marks = jnp.where(image_units == owner_ref[...], 1.0, 0.0)
+    before = jnp.where(
+        lax.broadcasted_iota(jnp.int32, (images, images), 0) < lax.broadcasted_iota(jnp.int32, (images, images), 1),
+        1.0,
+        0.0,
+    ).astype(bf16)
+    counts = jnp.dot(marks.astype(bf16), before, preferred_element_type=f32)
+    rank = jnp.sum(counts * marks, axis=0, keepdims=True).astype(jnp.int32)
+    slots_out = owner_ref[...] * capacity + rank
+    pick_t[...] = jnp.where(
+        lax.broadcasted_iota(jnp.int32, (slots, images), 0) == slots_out, 1.0, 0.0
+    ).astype(bf16)
+
+    for i in range(1, units):
+        v, device = unit_of(i)
+        remote(d1_src.at[slot_rows(v)], d1_dst.at[slot_rows(v)], d1_s.at[v], d1_r.at[v], device).wait_recv()
+    returned = lax.dot_general(pick_t[...], d1_dst[...], ROWS_TO_COLS, preferred_element_type=f32).astype(bf16)
+    d2_src[...] = returned
+    back[pl.ds(rows, images), my_cols] = returned
+
+    def head_cols(q):
+        return pl.ds(pl.multiple_of(q * cols, cols), cols)
+
+    def d2(i, source):
+        q, device = head_of(i)
+        return remote(d2_src, back.at[pl.ds(rows, images), head_cols(source)], d2_s.at[q], d2_r.at[source], device)
+
+    for i in range(1, tp):
+        d2(i, t).start()
+
+    @pl.when(carries & adjacent)
+    def _():
+        w_forward(base)
+
+    for i in range(1, tp):
+        d2(i, head_of(i)[0]).wait_recv()
+    for load in loads[3:]:
+        load.wait()
+
+    @pl.when(carries & adjacent)
+    def _():
+        w_forward(base + 1)
+
+    def p_copy(i):
+        at = pl.ds(pl.multiple_of(i * g_rows, g_rows), g_rows)
+        return remote(pa.at[at], pb.at[at], p_s.at[i], p_r.at[i], peer)
+
+    tile = 4 * g_rows
+
+    def p_step(j, carry):
+        at = pl.ds(pl.multiple_of(j * tile, tile), tile)
+        part = lax.dot_general(x[:, at], back[...], ROWS_TO_COLS, preferred_element_type=f32)
+        pf[at, :] = part
+
+        @pl.when(carries)
+        def _():
+            pa[at, :] = part.astype(bf16)
+            for k in range(tile // g_rows):
+                p_copy(j * (tile // g_rows) + k).start()
+
+        return carry
+
+    lax.fori_loop(0, columns // tile, p_step, 0)
+
+    forwarded = jnp.where(adjacent, base + early, 0)
+
+    def w_step(n):
+        @pl.when(carries & (n >= forwarded))
+        def _():
+            w_forward(n)
+
+        b, c = near_block(n // W_PARTS), lax.rem(n, W_PARTS)
+
+        @pl.when(jnp.logical_not(carries))
+        def _():
+            w_load(b, c).wait()
+
+        at = w_slice(b, c)
+        y[...] += jnp.dot(x[:, at], w[at, :], preferred_element_type=f32)
+
+        @pl.when(n == w_steps - 1)
+        def _():
+            c1_send()
+
+        gout[:, at] = lax.dot_general(back[...], w[at, :], COLS_TO_COLS, preferred_element_type=f32).astype(bf16)
+        for copy in grad_stores(n):
+            copy.start()
+
+    def grad_stores(n):
+        b, c = near_block(n // W_PARTS), lax.rem(n, W_PARTS)
+        at = w_slice(b, c)
+        return (
+            pltpu.make_async_copy(gout.at[pl.ds(0, rows), at], text_out.at[:, at], st.at[n]),
+            pltpu.make_async_copy(gout.at[pl.ds(rows, images), at], image_out.at[:, at], st.at[w_steps + n]),
+        )
+
+    text_rows, image_rows = pl.ds(0, rows), pl.ds(rows, images)
+
+    def c1(i, source, which, send, recv):
+        q, device = head_of(i)
+        return remote(yb.at[q, which], yr.at[source, which], send.at[q], recv.at[source], device)
+
+    def c1_send():
+        for q in range(tp):
+            yb[q] = y[:, q * cols : (q + 1) * cols].astype(bf16)
+        for i in range(1, tp):
+            c1(i, t, image_rows, ci_s, ci_r).start()
+        for i in range(1, tp):
+            c1(i, t, text_rows, ct_s, ct_r).start()
+
+    def c2(i):
+        v, device = unit_of(i)
+        return remote(c2_src.at[slot_rows(v)], c2_dst.at[slot_rows(me)], c2_s.at[v], c2_r.at[me], device)
+
+    def c2_send():
+        total = y[image_rows, my_cols]
+        for i in range(1, tp):
+            q = head_of(i)[0]
+            c1(i, q, image_rows, ci_s, ci_r).wait_recv()
+            total = total + yr[q, image_rows, :].astype(f32)
+        c2_src[...] = jnp.dot(pick_t[...], total.astype(bf16), preferred_element_type=f32).astype(bf16)
+        for i in range(1, units):
+            c2(i).start()
+        c2_dst[slot_rows(me), :] = c2_src[slot_rows(me), :]
+
+    def g_slice(b, c):
+        return pl.ds(pl.multiple_of(b * block + c * g_rows, g_rows), g_rows)
+
+    def chain_copies(b, c):
+        i, at = b * G_PARTS + c, g_slice(b, c)
+        return (
+            (z > z0 + b, remote(chain.at[at], above.at[at], ch_s.at[i], ab_r.at[i], (g, z - 1, t))),
+            (z < z0 + b, remote(chain.at[at], below.at[at], ch_s.at[i], be_r.at[i], (g, z + 1, t))),
+        )
+
+    def landing(c):
+        return landed.at[pl.ds(pl.multiple_of(c * g_rows, g_rows), g_rows)]
+
+    def result_copy(b, c, q):
+        return remote(
+            chain.at[g_slice(b, c), q * cols : (q + 1) * cols], landing(c), g_s.at[c * tp + q], g_r.at[c], (1 - g, z, q)
+        )
+
+    def g_step(m):
+        b, c = near_block(blocks - 1 - m // G_PARTS), lax.rem(m, G_PARTS)
+        i, at, zb = b * G_PARTS + c, g_slice(b, c), z0 + b
+        p_copy(i).wait_recv()
+        pf[at, :] += pb[at, :].astype(f32)
+
+        @pl.when((z >= zb) & (z < fsdp - 1))
+        def _():
+            remote(chain.at[at], above.at[at], ch_s.at[i], ab_r.at[i], peer).wait_recv()
+            pf[at, :] += above[at, :].astype(f32)
+
+        @pl.when((z <= zb) & (z > 0))
+        def _():
+            remote(chain.at[at], below.at[at], ch_s.at[i], be_r.at[i], peer).wait_recv()
+            pf[at, :] += below[at, :].astype(f32)
+
+        chain[at, :] = pf[at, :].astype(bf16)
+        for condition, copy in chain_copies(b, c):
+            pl.when(condition)(copy.start)
+
+        @pl.when(z == zb)
+        def _():
+            for q in range(tp):
+                result_copy(b, c, q).start()
+
+    ratio = g_steps // w_steps
+    turns = 2 * w_steps
+    sums = jnp.logical_not(carries)
+    w_at = jnp.where(sums & far_end, w_steps, 0)
+    g_at = jnp.where(far_end, 0, jnp.where(inside, w_steps, w_steps // 2 - 1))
+    c2_at = jnp.where(sums & inside, w_steps + w_steps // 2, jnp.where(sums & jnp.logical_not(far_end), w_steps + 1, turns - 1))
+
+    def turn(s, carry):
+        n, m = s - w_at, s - g_at
+
+        @pl.when(sums & (m >= 0) & (m < w_steps))
+        def _():
+            lax.fori_loop(0, ratio, lambda k, unused: (g_step(m * ratio + k), unused)[1], 0)
+
+        @pl.when((n >= 0) & (n < w_steps))
+        def _():
+            w_step(n)
+
+        @pl.when(s == c2_at)
+        def _():
+            c2_send()
+
+        return carry
+
+    lax.fori_loop(0, turns, turn, 0)
+
+    total = y[text_rows, my_cols]
+    for i in range(1, tp):
+        q = head_of(i)[0]
+        c1(i, q, text_rows, ct_s, ct_r).wait_recv()
+        total = total + yr[q, text_rows, :].astype(f32)
+    for i in range(1, units):
+        v, device = unit_of(i)
+        remote(c2_src.at[slot_rows(v)], c2_dst.at[slot_rows(v)], c2_s.at[v], c2_r.at[v], device).wait_recv()
+    placed = lax.dot_general(place_t[...], c2_dst[...], ROWS_TO_COLS, preferred_element_type=f32)
+    projected = jnp.where(is_img[...] > 0.5, placed, total) + bias_ref[...]
+    for s in range(rows // LENGTH):
+        values = projected[s * LENGTH : (s + 1) * LENGTH]
+        turned = values * cosv[...] + pltpu.roll(values, HALF, 1) * sinv[...]
+        keys[s * LENGTH : (s + 1) * LENGTH, :] = jnp.where(live(s), turned, 0.0).astype(bf16)
+    keys_store = pltpu.make_async_copy(keys, keys_out, ld.at[0])
+    keys_store.start()
+
+    for c in range(G_PARTS):
+        remote(landing(c), landing(c), g_s.at[0], g_r.at[c], peer).wait_recv()
+    wg[...] = landed[...].astype(f32) * (1.0 / rows)
+    wg_store = pltpu.make_async_copy(wg, wgrad_out, ld.at[1])
+    wg_store.start()
+
+    def each(count, body):
+        lax.fori_loop(0, count, lambda n, unused: (body(n), unused)[1], 0)
+
+    def w_sent(n):
+        b, c = n // W_PARTS, lax.rem(n, W_PARTS)
+        for condition, copy in w_routes(b, c):
+            pl.when(condition)(copy.wait_send)
+        w_send(b, c, peer, w_dd).wait_send()
+
+    @pl.when(carries)
+    def _():
+        each(w_steps, w_sent)
+        each(g_steps, lambda n: p_copy(n).wait_send())
+
+    def g_sent(n):
+        b, c = n // G_PARTS, lax.rem(n, G_PARTS)
+        for condition, copy in chain_copies(b, c):
+            pl.when(condition)(copy.wait_send)
+
+        @pl.when(z == z0 + b)
+        def _():
+            for q in range(tp):
+                result_copy(b, c, q).wait_send()
+
+    @pl.when(sums)
+    def _():
+        each(g_steps, g_sent)
+
+    for i in range(1, units):
+        d1(i).wait_send()
+        c2(i).wait_send()
+    for i in range(1, tp):
+        d2(i, t).wait_send()
+        c1(i, t, image_rows, ci_s, ci_r).wait_send()
+        c1(i, t, text_rows, ct_s, ct_r).wait_send()
+
+    def stored(n):
+        for copy in grad_stores(n):
+            copy.wait()
+
+    each(w_steps, stored)
+    keys_store.wait()
+    wg_store.wait()
+
+
+def rotary_tables():
+    frequency = ROPE_BASE ** (-(np.arange(HALF, dtype=np.float64) * 2.0) / HEAD_DIM)
+    table = np.arange(LENGTH, dtype=np.float64)[:, None] * frequency[None, :]
+    cosine, sine = np.cos(table), np.sin(table)
+    return (
+        np.concatenate([cosine, cosine], axis=1).astype(np.float32),
+        np.concatenate([-sine, sine], axis=1).astype(np.float32),
+    )
+
+
+def fits(groups, fsdp, tp, rows, head_cols, block):
+    units = groups * fsdp
+    if groups != 2 or units % tp or head_cols != HEAD_DIM or rows % LENGTH:
+        return False
+    blocks = units // tp
+    return blocks == 2 and fsdp % blocks == 0 and block % (G_PARTS * HEAD_DIM) == 0 and (rows // units) % 16 == 0
+
+
+def per_device(
+    text_embeds, image_embeds, key_weight, key_bias, key_cot, image_owner, image_slot, seq_lengths
+):
+    groups, fsdp, tp = lax.axis_size("group"), lax.axis_size("fsdp"), lax.axis_size("tp")
+    rows, columns = text_embeds.shape
+    images = image_embeds.shape[0]
+    cols = key_bias.shape[0]
+    block = key_weight.shape[0]
+    if not fits(groups, fsdp, tp, rows, cols, block):
+        return per_device_plain(
+            text_embeds, image_embeds, key_weight, key_bias, key_cot, image_owner, image_slot, seq_lengths
+        )
+    units = groups * fsdp
+    capacity = rows // units
+    slots = units * capacity
+    both, key_cols = rows + images, cols * tp
+    blocks = units // tp
+    w_steps, g_steps = blocks * W_PARTS, blocks * G_PARTS
+    cosine, sine = rotary_tables()
+    bf16, f32 = jnp.bfloat16, jnp.float32
+    hbm = pl.BlockSpec(memory_space=pl.ANY)
+    vmem = pl.BlockSpec(memory_space=pltpu.VMEM)
+    dma = lambda n: pltpu.SemaphoreType.DMA((n,))
+    return pl.pallas_call(
+        functools.partial(fused_kernel, groups, fsdp, tp, capacity),
+        out_shape=(
+            jax.ShapeDtypeStruct((rows, cols), bf16),
+            jax.ShapeDtypeStruct((rows, columns), bf16),
+            jax.ShapeDtypeStruct((images, columns), bf16),
+            jax.ShapeDtypeStruct((block, cols), f32),
+        ),
+        in_specs=[hbm, hbm, hbm, vmem, hbm, vmem, vmem, vmem, hbm, hbm],
+        out_specs=(hbm, hbm, hbm, hbm),
+        scratch_shapes=[
+            pltpu.VMEM((both, columns), bf16),
+            pltpu.VMEM((columns, key_cols), bf16),
+            pltpu.VMEM((rows, key_cols), bf16),
+            pltpu.VMEM((LENGTH, cols), f32),
+            pltpu.VMEM((LENGTH, cols), f32),
+            pltpu.VMEM((both, key_cols), bf16),
+            pltpu.VMEM((slots, images), bf16),
+            pltpu.VMEM((slots, rows), bf16),
+            pltpu.VMEM((rows, cols), f32),
+            pltpu.VMEM((slots, cols), bf16),
+            pltpu.VMEM((slots, cols), bf16),
+            pltpu.VMEM((images, cols), bf16),
+            pltpu.VMEM((columns, key_cols), f32),
+            pltpu.VMEM((columns, key_cols), bf16),
+            pltpu.VMEM((columns, key_cols), bf16),
+            pltpu.VMEM((columns, key_cols), bf16),
+            pltpu.VMEM((columns, key_cols), bf16),
+            pltpu.VMEM((columns, key_cols), bf16),
+            pltpu.VMEM((both, key_cols), f32),
+            pltpu.VMEM((tp, both, cols), bf16),
+            pltpu.VMEM((tp, both, cols), bf16),
+            pltpu.VMEM((slots, cols), bf16),
+            pltpu.VMEM((slots, cols), bf16),
+            pltpu.VMEM((both, columns), bf16),
+            pltpu.VMEM((block, cols), bf16),
+            pltpu.VMEM((block, cols), f32),
+            pltpu.VMEM((rows, cols), bf16),
+            dma(5), dma(w_steps), dma(w_steps), dma(w_steps), dma(w_steps),
+            dma(units), dma(units), dma(tp), dma(tp),
+            dma(tp), dma(tp), dma(tp), dma(tp), dma(units), dma(units),
+            dma(g_steps), dma(g_steps), dma(g_steps), dma(g_steps), dma(g_steps),
+            dma(G_PARTS * tp), dma(G_PARTS), dma(2 * w_steps),
+        ],
+        compiler_params=pltpu.CompilerParams(
+            collective_id=0, has_side_effects=True, vmem_limit_bytes=60 * 1024 * 1024
+        ),
+        name="fused",
+    )(
+        text_embeds, image_embeds, key_weight, key_bias.reshape(1, -1), key_cot,
+        image_owner.reshape(1, -1), image_slot.reshape(1, -1), seq_lengths.reshape(1, -1), cosine, sine,
+    )
+
+
 def solution(mesh):
     in_specs = (
         P(("group", "fsdp"), "tp"),

time: 137 us -> 62.2 us (0.45)
  the two profiles are of different devices: /device:TPU:3 before, /device:TPU:0 now
where the time goes in v1:
time: 62.2 us; the launch traced here: 61.3 us
  Pallas kernels  54.1 us (87%)
  local copies, waits for them, and re-layouts  6.62 us (11%)
  between operations  0.65 us (1%)
    pallas_call x1, Pallas kernels, per_device(): pl.pallas_call(functools.partial(fused_kernel, groups, fsdp, tp, capacity...  54.1 us
    unnamed x8, local copies, waits for them, and re-layouts  6.62 us

profile of v1, /device:TPU:0, one launch (start us, length us, event | category | flops | bytes accessed | tf_op | source)
XLA Modules:
  0.0 61.3 jit_solution(9998382962689774459)
XLA Ops:
  0.6 54.1 %fused.1 = (bf16[512,128]{1,0:T(8,128)(2,1)}, bf16[512,2048]{1,0:T(8,128)(2,1)}, bf16[256,2048]{1,0:T(8,128)(2,1)}, f32[1024,128]{1,0:T(8,128)}) custom-call(bf16[512,2048]{1,0:T(8,128)(2,1)} %text_ref.1, bf16[256,2048]{1,0:T(8,128)(2,1)} %image_ref.1, bf16[1024,512]{1,0:T(8,128)(2,1)} %weight_ref.1, f32[1,128]{1,0:T(1,128)} %bitcast.6, ...), custom_call_target="tpu_custom_call" | custom-call | tf_op jit(solution)/shard_map/fused/pallas_call | solution.py:698
  54.7 1.6 %copy.18 = bf16[512,128]{1,0:T(8,128)(2,1)} copy(bf16[512,128]{1,0:T(8,128)(2,1)} %get-tuple-element.8) | data formatting | bytes 262144
  56.3 0.0 copy-start
  56.3 0.0 copy-start.1
  56.3 3.3 %copy.19 = bf16[512,2048]{1,0:T(8,128)(2,1)} copy(bf16[512,2048]{1,0:T(8,128)(2,1)} %get-tuple-element.9) | data formatting | bytes 4194304
  59.5 0.0 copy-done
  59.5 1.0 %copy.20 = bf16[256,2048]{1,0:T(8,128)(2,1)} copy(bf16[256,2048]{1,0:T(8,128)(2,1)S(1)} %copy-done) | data formatting | bytes 2097152
  60.5 0.0 copy-done.1
  60.5 0.8 %copy.21 = f32[1024,128]{1,0:T(8,128)} copy(f32[1024,128]{1,0:T(8,128)S(1)} %copy-done.1) | data formatting | bytes 1048576
Async XLA Ops:
  56.3 3.3 %copy-start = (bf16[256,2048]{1,0:T(8,128)(2,1)S(1)}, bf16[256,2048]{1,0:T(8,128)(2,1)}, u32[]{:S(2)}) copy-start(bf16[256,2048]{1,0:T(8,128)(2,1)} %get-tuple-element.10) | copy-start | bytes 3145732
  56.3 4.3 %copy-start.1 = (f32[1024,128]{1,0:T(8,128)S(1)}, f32[1024,128]{1,0:T(8,128)}, u32[]{:S(2)}) copy-start(f32[1024,128]{1,0:T(8,128)} %get-tuple-element.11) | copy-start | bytes 1572868

commit v2 on v1

--- a/solution.py
+++ b/solution.py
@@ -248,12 +248,12 @@
 
 def fused_kernel(
     groups, fsdp, tp, capacity,
-    text_ref, image_ref, weight_ref, bias_ref, cot_ref, owner_ref, slot_ref, lens_ref, cos_ref, sin_ref,
+    text_ref, image_ref, weight_ref, bias_hbm, cot_ref, owner_hbm, slot_hbm, lens_hbm, cos_ref, sin_ref,
     keys_out, text_out, image_out, wgrad_out,
-    x, w, cot, cosv, sinv, back, pick_t, place_t, is_img,
-    d1_src, d1_dst, d2_src, pf, pa, pb, chain, above, below, y, yb, yr, c2_src, c2_dst, gout, landed, wg, keys,
+    bias_ref, owner_ref, slot_ref, lens_ref, x, w, cot, cosv, sinv, back, pick_t, place_t, is_img,
+    d1_src, d1_dst, d2_src, pf, pa, pb, chain, above, below, y, yb, yr, c2_src, c2_dst, landed,
     ld, w_recv, w_up, w_dn, w_dd, d1_s, d1_r, d2_s, d2_r, ci_s, ci_r, ct_s, ct_r, c2_s, c2_r,
-    p_s, p_r, ab_r, be_r, ch_s, g_s, g_r, st,
+    p_s, p_r, ab_r, be_r, ch_s, g_s, g_r,
 ):
     f32, bf16 = jnp.float32, jnp.bfloat16
     g, z, t = lax.axis_index("group"), lax.axis_index("fsdp"), lax.axis_index("tp")
@@ -302,14 +302,19 @@
         for core in range(groups):
             pl.semaphore_signal(barrier, inc=1, device_id=(core, z, q), device_id_type=MESH)
 
-    loads = [
-        pltpu.make_async_copy(cot_ref, cot, ld.at[0]),
-        pltpu.make_async_copy(cos_ref, cosv, ld.at[1]),
-        pltpu.make_async_copy(sin_ref, sinv, ld.at[2]),
-        pltpu.make_async_copy(text_ref, x.at[pl.ds(0, rows)], ld.at[3]),
-        pltpu.make_async_copy(image_ref, x.at[pl.ds(rows, images)], ld.at[4]),
-    ]
-    for load in loads[:3]:
+    pairs = (
+        (slot_hbm, slot_ref),
+        (cot_ref, cot),
+        (cos_ref, cosv),
+        (sin_ref, sinv),
+        (lens_hbm, lens_ref),
+        (owner_hbm, owner_ref),
+        (bias_hbm, bias_ref),
+        (text_ref, x.at[pl.ds(0, rows)]),
+        (image_ref, x.at[pl.ds(rows, images)]),
+    )
+    loads = [pltpu.make_async_copy(source, target, ld.at[i]) for i, (source, target) in enumerate(pairs)]
+    for load in loads[:5]:
         load.start()
 
     def w_slice(b, c):
@@ -325,9 +330,10 @@
         for c in range(W_PARTS):
             w_load(z - z0, c).start()
 
-    for load in loads[3:]:
+    for load in loads[5:]:
         load.start()
 
+    loads[0].wait()
     slot_ids = lax.broadcasted_iota(jnp.int32, (slots, rows), 0)
     place_t[...] = jnp.where(slot_ids == slot_ref[...], 1.0, 0.0).astype(bf16)
     is_img[...] = lax.dot_general(
@@ -343,7 +349,7 @@
         values = jnp.where(live(s), cot[span, at].astype(f32), 0.0)
         return values * cosv[...] - pltpu.roll(values, HALF, 1) * sinv[...]
 
-    for load in loads[:3]:
+    for load in loads[1:5]:
         load.wait()
     mine = jnp.concatenate([rotated_back(s, my_cols) for s in range(rows // LENGTH)], axis=0).astype(bf16)
     d1_src[...] = jnp.dot(place_t[...], mine, preferred_element_type=f32).astype(bf16)
@@ -391,6 +397,7 @@
         for h in range(tp):
             at = pl.ds(h * cols, cols)
             back[span, at] = jnp.where(is_img[span, :] > 0.5, 0.0, rotated_back(s, at)).astype(bf16)
+    loads[5].wait()
     image_units = lax.broadcasted_iota(jnp.int32, (units, images), 0)
     marks = jnp.where(image_units == owner_ref[...], 1.0, 0.0)
     before = jnp.where(
@@ -428,7 +435,7 @@
 
     for i in range(1, tp):
         d2(i, head_of(i)[0]).wait_recv()
-    for load in loads[3:]:
+    for load in loads[6:]:
         load.wait()
 
     @pl.when(carries & adjacent)
@@ -476,17 +483,9 @@
         def _():
             c1_send()
 
-        gout[:, at] = lax.dot_general(back[...], w[at, :], COLS_TO_COLS, preferred_element_type=f32).astype(bf16)
-        for copy in grad_stores(n):
-            copy.start()
-
-    def grad_stores(n):
-        b, c = near_block(n // W_PARTS), lax.rem(n, W_PARTS)
-        at = w_slice(b, c)
-        return (
-            pltpu.make_async_copy(gout.at[pl.ds(0, rows), at], text_out.at[:, at], st.at[n]),
-            pltpu.make_async_copy(gout.at[pl.ds(rows, images), at], image_out.at[:, at], st.at[w_steps + n]),
-        )
+        grads = lax.dot_general(back[...], w[at, :], COLS_TO_COLS, preferred_element_type=f32).astype(bf16)
+        text_out[:, at] = grads[:rows]
+        image_out[:, at] = grads[rows:]
 
     text_rows, image_rows = pl.ds(0, rows), pl.ds(rows, images)
 
@@ -599,15 +598,11 @@
     for s in range(rows // LENGTH):
         values = projected[s * LENGTH : (s + 1) * LENGTH]
         turned = values * cosv[...] + pltpu.roll(values, HALF, 1) * sinv[...]
-        keys[s * LENGTH : (s + 1) * LENGTH, :] = jnp.where(live(s), turned, 0.0).astype(bf16)
-    keys_store = pltpu.make_async_copy(keys, keys_out, ld.at[0])
-    keys_store.start()
+        keys_out[s * LENGTH : (s + 1) * LENGTH, :] = jnp.where(live(s), turned, 0.0).astype(bf16)
 
     for c in range(G_PARTS):
         remote(landing(c), landing(c), g_s.at[0], g_r.at[c], peer).wait_recv()
-    wg[...] = landed[...].astype(f32) * (1.0 / rows)
-    wg_store = pltpu.make_async_copy(wg, wgrad_out, ld.at[1])
-    wg_store.start()
+    wgrad_out[...] = landed[...].astype(f32) * (1.0 / rows)
 
     def each(count, body):
         lax.fori_loop(0, count, lambda n, unused: (body(n), unused)[1], 0)
@@ -645,13 +640,14 @@
         c1(i, t, image_rows, ci_s, ci_r).wait_send()
         c1(i, t, text_rows, ct_s, ct_r).wait_send()
 
-    def stored(n):
-        for copy in grad_stores(n):
-            copy.wait()
-
-    each(w_steps, stored)
-    keys_store.wait()
-    wg_store.wait()
+
+def write_kernel(*refs):
+    count = (len(refs) - 1) // 2
+    copies = [pltpu.make_async_copy(refs[i], refs[count + i], refs[-1].at[i]) for i in range(count)]
+    for copy in copies:
+        copy.start()
+    for copy in copies:
+        copy.wait()
 
 
 def rotary_tables():
@@ -692,20 +688,29 @@
     w_steps, g_steps = blocks * W_PARTS, blocks * G_PARTS
     cosine, sine = rotary_tables()
     bf16, f32 = jnp.bfloat16, jnp.float32
-    hbm = pl.BlockSpec(memory_space=pl.ANY)
+    hbm = pl.BlockSpec(memory_space=pltpu.HBM)
     vmem = pl.BlockSpec(memory_space=pltpu.VMEM)
     dma = lambda n: pltpu.SemaphoreType.DMA((n,))
-    return pl.pallas_call(
+    shapes = (
+        jax.ShapeDtypeStruct((rows, cols), bf16),
+        jax.ShapeDtypeStruct((rows, columns), bf16),
+        jax.ShapeDtypeStruct((images, columns), bf16),
+        jax.ShapeDtypeStruct((block, cols), f32),
+    )
+    operands = (
+        text_embeds, image_embeds, key_weight, key_bias.reshape(1, -1), key_cot,
+        image_owner.reshape(1, -1), image_slot.reshape(1, -1), seq_lengths.reshape(1, -1), jnp.asarray(cosine), jnp.asarray(sine),
+    )
+    held = pl.pallas_call(
         functools.partial(fused_kernel, groups, fsdp, tp, capacity),
-        out_shape=(
-            jax.ShapeDtypeStruct((rows, cols), bf16),
-            jax.ShapeDtypeStruct((rows, columns), bf16),
-            jax.ShapeDtypeStruct((images, columns), bf16),
-            jax.ShapeDtypeStruct((block, cols), f32),
-        ),
-        in_specs=[hbm, hbm, hbm, vmem, hbm, vmem, vmem, vmem, hbm, hbm],
-        out_specs=(hbm, hbm, hbm, hbm),
+        out_shape=tuple(pltpu.VMEM(leaf.shape, leaf.dtype) for leaf in shapes),
+        in_specs=[hbm] * 10,
+        out_specs=(vmem, vmem, vmem, vmem),
         scratch_shapes=[
+            pltpu.VMEM((1, cols), f32),
+            pltpu.VMEM((1, images), jnp.int32),
+            pltpu.VMEM((1, rows), jnp.int32),
+            pltpu.VMEM((1, seq_lengths.shape[0]), jnp.int32),
             pltpu.VMEM((both, columns), bf16),
             pltpu.VMEM((columns, key_cols), bf16),
             pltpu.VMEM((rows, key_cols), bf16),
@@ -729,24 +734,27 @@
             pltpu.VMEM((tp, both, cols), bf16),
             pltpu.VMEM((slots, cols), bf16),
             pltpu.VMEM((slots, cols), bf16),
-            pltpu.VMEM((both, columns), bf16),
             pltpu.VMEM((block, cols), bf16),
-            pltpu.VMEM((block, cols), f32),
-            pltpu.VMEM((rows, cols), bf16),
-            dma(5), dma(w_steps), dma(w_steps), dma(w_steps), dma(w_steps),
+            dma(9), dma(w_steps), dma(w_steps), dma(w_steps), dma(w_steps),
             dma(units), dma(units), dma(tp), dma(tp),
             dma(tp), dma(tp), dma(tp), dma(tp), dma(units), dma(units),
             dma(g_steps), dma(g_steps), dma(g_steps), dma(g_steps), dma(g_steps),
-            dma(G_PARTS * tp), dma(G_PARTS), dma(2 * w_steps),
+            dma(G_PARTS * tp), dma(G_PARTS),
         ],
         compiler_params=pltpu.CompilerParams(
-            collective_id=0, has_side_effects=True, vmem_limit_bytes=60 * 1024 * 1024
+            collective_id=0, has_side_effects=True, vmem_limit_bytes=44 * 1024 * 1024
         ),
         name="fused",
-    )(
-        text_embeds, image_embeds, key_weight, key_bias.reshape(1, -1), key_cot,
-        image_owner.reshape(1, -1), image_slot.reshape(1, -1), seq_lengths.reshape(1, -1), cosine, sine,
-    )
+    )(*(pltpu.with_memory_space_constraint(operand, pltpu.HBM) for operand in operands))
+    return pl.pallas_call(
+        write_kernel,
+        out_shape=shapes,
+        in_specs=[vmem] * 4,
+        out_specs=(pl.BlockSpec(memory_space=pl.ANY),) * 4,
+        scratch_shapes=[dma(4)],
+        compiler_params=pltpu.CompilerParams(vmem_limit_bytes=4 * 1024 * 1024),
+        name="write",
+    )(*held)
 
 
 def solution(mesh):

time: 62.2 us -> 56.4 us (0.907)
  local copies, waits for them, and re-layouts: 6.62 us -> 0 us
  Pallas kernels: 54.1 us -> 54.9 us
    unnamed x8 -> x0, local copies, waits for them, and re-layouts: 6.62 us -> none
    pallas_call x0 -> x1, Pallas kernels: none -> 1.91 us  [per_device(): pl.pallas_call(write_kernel, out_shape=shapes, in_specs=[vmem] * 4, out_s...]
    pallas_call x1, Pallas kernels: 54.1 us -> 53 us  [per_device(): pl.pallas_call(functools.partial(fused_kernel, groups, fsdp, tp, capacity...]
where the time goes in v2:
time: 56.4 us; the launch traced here: 55.5 us
  Pallas kernels  54.9 us (97%)
  between operations  0.64 us (1%)
    pallas_call x1, Pallas kernels, per_device(): pl.pallas_call(functools.partial(fused_kernel, groups, fsdp, tp, capacity...  53 us
    pallas_call x1, Pallas kernels, per_device(): pl.pallas_call(write_kernel, out_shape=shapes, in_specs=[vmem] * 4, out_s...  1.91 us

profile of v2, /device:TPU:0, one launch (start us, length us, event | category | flops | bytes accessed | tf_op | source)
XLA Modules:
  0.0 55.5 jit_solution(13621083731099002850)
XLA Ops:
  0.6 53.0 %fused.1 = (bf16[512,128]{1,0:T(8,128)(2,1)S(1)}, bf16[512,2048]{1,0:T(8,128)(2,1)S(1)}, bf16[256,2048]{1,0:T(8,128)(2,1)S(1)}, f32[1024,128]{1,0:T(8,128)S(1)}) custom-call(bf16[512,2048]{1,0:T(8,128)(2,1)} %text_ref.1, bf16[256,2048]{1,0:T(8,128)(2,1)} %image_ref.1, bf16[1024,512]{1,0:T(8,128)(2,1)} %weight_ref.1, f32[1,128]{1,0:T(1,128)} %bitcast.6, ...), custom_call_target="tpu_custom_call" | custom-call | tf_op jit(solution)/shard_map/fused/pallas_call | solution.py:704
  53.6 1.9 %write.1 = (bf16[512,128]{1,0:T(8,128)(2,1)}, bf16[512,2048]{1,0:T(8,128)(2,1)}, bf16[256,2048]{1,0:T(8,128)(2,1)}, f32[1024,128]{1,0:T(8,128)}) custom-call(bf16[512,128]{1,0:T(8,128)(2,1)S(1)} %get-tuple-element.8.refs_0_, bf16[512,2048]{1,0:T(8,128)(2,1)S(1)} %get-tuple-element.9.refs_1_, bf16[256,2048]{1,0:T(8,128)(2,1)S(1)} %get-tuple-element.10.refs_2_, ...), custom_call_target="tpu_custom_call" | custom-call | tf_op jit(solution)/shard_map/write/pallas_call | solution.py:749

commit v3 on v2

--- a/solution.py
+++ b/solution.py
@@ -243,7 +243,9 @@
 ROWS_TO_COLS = (((0,), (0,)), ((), ()))
 COLS_TO_COLS = (((1,), (1,)), ((), ()))
 W_PARTS = 4
+W_MAIN = 3
 G_PARTS = 8
+G_MAIN = 6
 
 
 def fused_kernel(
@@ -251,9 +253,9 @@
     text_ref, image_ref, weight_ref, bias_hbm, cot_ref, owner_hbm, slot_hbm, lens_hbm, cos_ref, sin_ref,
     keys_out, text_out, image_out, wgrad_out,
     bias_ref, owner_ref, slot_ref, lens_ref, x, w, cot, cosv, sinv, back, pick_t, place_t, is_img,
-    d1_src, d1_dst, d2_src, pf, pa, pb, chain, above, below, y, yb, yr, c2_src, c2_dst, landed,
+    d1_src, d1_dst, d2_src, pf, pa, pb, chain, above, below, y, yb, yr, c2_src, c2_dst, landed, side,
     ld, w_recv, w_up, w_dn, w_dd, d1_s, d1_r, d2_s, d2_r, ci_s, ci_r, ct_s, ct_r, c2_s, c2_r,
-    p_s, p_r, ab_r, be_r, ch_s, g_s, g_r,
+    p_s, p_r, ab_r, be_r, ch_s, g_s, g_r, x_s, x_r, h_r, h_z, h_x,
 ):
     f32, bf16 = jnp.float32, jnp.bfloat16
     g, z, t = lax.axis_index("group"), lax.axis_index("fsdp"), lax.axis_index("tp")
@@ -276,10 +278,25 @@
     adjacent = inside | (z == z0 - 1) | (z == z0 + blocks)
     my_cols = pl.ds(pl.multiple_of(t * cols, cols), cols)
     peer = (1 - g, z, t)
+    other = lax.bitwise_xor(t, 1)
+    beside = (g, z, other)
+    other_z0 = fsdp - blocks - z0
+    upward = z0 > 0
+    entry = jnp.where(upward, z == z0, z == z0 + blocks - 1)
+    border = jnp.where(upward, z == z0 - 1, z == z0 + blocks)
 
     def near_block(k):
         within = lax.rem(z - z0 + k + blocks, blocks)
         return jnp.where(inside, within, jnp.where(z < z0, k, blocks - 1 - k))
+
+    def far_other(k):
+        within = lax.rem(z - other_z0 + blocks - 1 - k + blocks, blocks)
+        return jnp.where(inside, jnp.where(upward, k, blocks - 1 - k), within)
+
+    def w_part(n):
+        late = n >= blocks * W_MAIN
+        k = jnp.where(late, n - blocks * W_MAIN, n // W_MAIN)
+        return near_block(k), jnp.where(late, W_MAIN, lax.rem(n, W_MAIN))
 
     def unit_of(i):
         v = lax.rem(me + i, units)
@@ -330,6 +347,13 @@
         for c in range(W_PARTS):
             w_load(z - z0, c).start()
 
+    def side_load(b):
+        return pltpu.make_async_copy(weight_ref.at[pl.ds(W_MAIN * w_rows, w_rows)], side.at[b], h_r.at[b])
+
+    @pl.when(carries & jnp.logical_not(inside))
+    def _():
+        side_load(z - other_z0).start()
+
     for load in loads[5:]:
         load.start()
 
@@ -361,7 +385,11 @@
 
     def d1(i):
         v, device = unit_of(i)
-        return remote(d1_src.at[slot_rows(v)], d1_dst.at[slot_rows(me)], d1_s.at[v], d1_r.at[me], device)
+        return remote(d1_src.at[slot_rows(v)], d1_dst.at[slot_rows(me)], d1_s, d1_r, device)
+
+    def d1_all():
+        at = pl.ds(0, (units - 1) * capacity)
+        return remote(d1_src.at[at], d1_dst.at[at], d1_s, d1_r, peer)
 
     for i in range(1, units):
         d1(i).start()
@@ -371,25 +399,54 @@
         i = b * W_PARTS + c
         return remote(w.at[w_slice(b, c)], w.at[w_slice(b, c)], sem.at[i], w_recv.at[i], to)
 
+    def w_share(b, c):
+        return remote(w.at[w_slice(b, c)], w.at[w_slice(b, c)], w_dd, w_recv.at[b * W_PARTS + c], peer)
+
     def w_routes(b, c):
         return (
-            ((z >= z0 + b) & (z < fsdp - 1), w_send(b, c, (g, z + 1, t), w_up)),
-            ((z <= z0 + b) & (z > 0), w_send(b, c, (g, z - 1, t), w_dn)),
+            ((z >= z0 + b) & (z < fsdp - 1) & ((c < W_MAIN) | (z + 1 < z0 + blocks)), w_send(b, c, (g, z + 1, t), w_up)),
+            ((z <= z0 + b) & (z > 0) & ((c < W_MAIN) | (z > z0)), w_send(b, c, (g, z - 1, t), w_dn)),
         )
 
-    def w_forward(n):
-        b, c = near_block(n // W_PARTS), lax.rem(n, W_PARTS)
+    def w_inward(c):
+        b = z - z0
+        return (
+            (upward, w_send(b, c, (g, z + 1, t), w_up)),
+            (jnp.logical_not(upward), w_send(b, c, (g, z - 1, t), w_dn)),
+        )
+
+    def side_routes(b):
+        step = jnp.where(upward, 1, -1)
+        at = w_slice(b, W_MAIN)
+        return (
+            ((z + step >= 0) & (z + step < fsdp), remote(side.at[b], side.at[b], h_z.at[b], h_r.at[b], (g, z + step, t))),
+            (inside, remote(side.at[b], w.at[at], h_x.at[b], w_recv.at[b * W_PARTS + W_MAIN], beside)),
+        )
+
+    def side_forward(b):
+        side_load(b).wait()
+        for condition, copy in side_routes(b):
+            pl.when(condition)(copy.start)
+
+    def side_block(k):
+        return jnp.where(upward, blocks - 1 - k, k)
+
+    def w_forward(b, c):
         w_load(b, c).wait()
-        for condition, copy in w_routes(b, c):
-            pl.when(condition)(copy.start)
-        w_send(b, c, peer, w_dd).start()
+        held = entry & (z == z0 + b) & (c >= 2)
+        for (condition, copy), inward in zip(w_routes(b, c), (upward, jnp.logical_not(upward))):
+            pl.when(condition & jnp.logical_not(held & inward))(copy.start)
+        w_share(b, c).start()
 
     @pl.when(carries & inside)
     def _():
-        lax.fori_loop(0, W_PARTS, lambda n, carry: (w_forward(n), carry)[1], 0)
-
-    base = jnp.where(inside, W_PARTS, 0)
-    early = 2
+        lax.fori_loop(0, W_PARTS, lambda c, carry: (w_forward(z - z0, c), carry)[1], 0)
+
+    @pl.when(carries & jnp.logical_not(inside))
+    def _():
+        side_forward(z - other_z0)
+
+    base = jnp.where(inside, W_MAIN, 0)
 
     y[...] = jnp.zeros_like(y)
     for s in range(rows // LENGTH):
@@ -412,9 +469,19 @@
         lax.broadcasted_iota(jnp.int32, (slots, images), 0) == slots_out, 1.0, 0.0
     ).astype(bf16)
 
-    for i in range(1, units):
-        v, device = unit_of(i)
-        remote(d1_src.at[slot_rows(v)], d1_dst.at[slot_rows(v)], d1_s.at[v], d1_r.at[v], device).wait_recv()
+    tile = block // 2
+    loads[7].wait()
+
+    def p_text(j, carry):
+        at = pl.ds(pl.multiple_of(j * tile, tile), tile)
+        pf[at, :] = lax.dot_general(
+            x[0:rows, at], back[0:rows, :], ROWS_TO_COLS, preferred_element_type=f32
+        )
+        return carry
+
+    lax.fori_loop(0, columns // tile, p_text, 0)
+
+    d1_all().wait_recv()
     returned = lax.dot_general(pick_t[...], d1_dst[...], ROWS_TO_COLS, preferred_element_type=f32).astype(bf16)
     d2_src[...] = returned
     back[pl.ds(rows, images), my_cols] = returned
@@ -424,106 +491,154 @@
 
     def d2(i, source):
         q, device = head_of(i)
-        return remote(d2_src, back.at[pl.ds(rows, images), head_cols(source)], d2_s.at[q], d2_r.at[source], device)
+        return remote(d2_src, back.at[pl.ds(rows, images), head_cols(source)], d2_s, d2_r, device)
+
+    text_rows, image_rows = pl.ds(0, rows), pl.ds(rows, images)
+
+    def d2_all():
+        at = pl.ds(0, tp - 1)
+        return remote(yb.at[at, image_rows], yr.at[at, image_rows], d2_s, d2_r, peer)
 
     for i in range(1, tp):
         d2(i, t).start()
 
     @pl.when(carries & adjacent)
     def _():
-        w_forward(base)
-
-    for i in range(1, tp):
-        d2(i, head_of(i)[0]).wait_recv()
-    for load in loads[6:]:
-        load.wait()
+        w_forward(*w_part(base))
+
+    @pl.when(carries & (border | entry))
+    def _():
+        side_forward(side_block(jnp.where(border, 1, 0)))
+
+    d2_all().wait_recv()
+    loads[6].wait()
+    loads[8].wait()
 
     @pl.when(carries & adjacent)
     def _():
-        w_forward(base + 1)
+        w_forward(*w_part(base + 1))
+
+    @pl.when(carries & entry)
+    def _():
+        for c in range(2, W_PARTS):
+            for condition, copy in w_inward(c):
+                pl.when(condition)(copy.start)
 
     def p_copy(i):
         at = pl.ds(pl.multiple_of(i * g_rows, g_rows), g_rows)
-        return remote(pa.at[at], pb.at[at], p_s.at[i], p_r.at[i], peer)
-
-    tile = 4 * g_rows
-
-    def p_step(j, carry):
+        return remote(pa.at[at], pb.at[at], p_s, p_r.at[i], peer)
+
+    def g_slice(b, c):
+        return pl.ds(pl.multiple_of(b * block + c * g_rows, g_rows), g_rows)
+
+    def x_copy(b, c):
+        i, at = b * G_PARTS + c, g_slice(b, c)
+        return remote(pb.at[at], pa.at[at], x_s, x_r.at[i], beside)
+
+    def x_send(b, c):
+        i, at = b * G_PARTS + c, g_slice(b, c)
+        p_copy(i).wait_recv()
+        pb[at, :] = (pf[at, :] + pb[at, :].astype(f32)).astype(bf16)
+        x_copy(b, c).start()
+
+    def p_step(k, carry):
+        b, half = near_block(blocks - 1 - k // 2), 1 - lax.rem(k, 2)
+        j = b * 2 + half
         at = pl.ds(pl.multiple_of(j * tile, tile), tile)
-        part = lax.dot_general(x[:, at], back[...], ROWS_TO_COLS, preferred_element_type=f32)
+        part = pf[at, :] + lax.dot_general(
+            x[rows:both, at], back[rows:both, :], ROWS_TO_COLS, preferred_element_type=f32
+        )
         pf[at, :] = part
 
         @pl.when(carries)
         def _():
             pa[at, :] = part.astype(bf16)
-            for k in range(tile // g_rows):
-                p_copy(j * (tile // g_rows) + k).start()
+            for c in range(tile // g_rows):
+                p_copy(j * (tile // g_rows) + c).start()
+
+        @pl.when(jnp.logical_not(carries) & (half == 0))
+        def _():
+            lax.fori_loop(G_MAIN, G_PARTS, lambda c, unused: (x_send(b, c), unused)[1], 0)
 
         return carry
 
     lax.fori_loop(0, columns // tile, p_step, 0)
 
-    forwarded = jnp.where(adjacent, base + early, 0)
+    @pl.when(carries & adjacent)
+    def _():
+        w_forward(*w_part(base + 2))
+
+    @pl.when(carries & inside)
+    def _():
+        side_forward(side_block(jnp.where(entry, 1, 0)))
 
     def w_step(n):
-        @pl.when(carries & (n >= forwarded))
-        def _():
-            w_forward(n)
-
-        b, c = near_block(n // W_PARTS), lax.rem(n, W_PARTS)
+        b, c = w_part(n)
+        ahead = jnp.where(border, n + 3, n)
+        next_b, next_c = w_part(ahead)
+        forwarded = (adjacent & (ahead >= base) & (ahead < base + 3)) | (inside & (z == z0 + next_b))
+
+        @pl.when(carries & (ahead < w_steps) & jnp.logical_not(forwarded))
+        def _():
+            w_forward(next_b, next_c)
 
         @pl.when(jnp.logical_not(carries))
         def _():
             w_load(b, c).wait()
 
         at = w_slice(b, c)
-        y[...] += jnp.dot(x[:, at], w[at, :], preferred_element_type=f32)
-
-        @pl.when(n == w_steps - 1)
-        def _():
-            c1_send()
+        for which, send, recv in ((image_rows, ci_s, ci_r), (text_rows, ct_s, ct_r)):
+            y[which, :] += jnp.dot(x[which, at], w[at, :], preferred_element_type=f32)
+
+            @pl.when(n == w_steps - 1)
+            def _():
+                c1_send(which, send, recv)
 
         grads = lax.dot_general(back[...], w[at, :], COLS_TO_COLS, preferred_element_type=f32).astype(bf16)
         text_out[:, at] = grads[:rows]
         image_out[:, at] = grads[rows:]
 
-    text_rows, image_rows = pl.ds(0, rows), pl.ds(rows, images)
-
     def c1(i, source, which, send, recv):
         q, device = head_of(i)
-        return remote(yb.at[q, which], yr.at[source, which], send.at[q], recv.at[source], device)
-
-    def c1_send():
+        return remote(yb.at[q, which], yr.at[source, which], send, recv, device)
+
+    def c1_all(which, send, recv):
+        at = pl.ds(0, tp - 1)
+        return remote(yb.at[at, which], yr.at[at, which], send, recv, peer)
+
+    def c1_send(which, send, recv):
         for q in range(tp):
-            yb[q] = y[:, q * cols : (q + 1) * cols].astype(bf16)
+            yb[q, which, :] = y[which, q * cols : (q + 1) * cols].astype(bf16)
         for i in range(1, tp):
-            c1(i, t, image_rows, ci_s, ci_r).start()
-        for i in range(1, tp):
-            c1(i, t, text_rows, ct_s, ct_r).start()
+            c1(i, t, which, send, recv).start()
 
     def c2(i):
         v, device = unit_of(i)
-        return remote(c2_src.at[slot_rows(v)], c2_dst.at[slot_rows(me)], c2_s.at[v], c2_r.at[me], device)
+        return remote(c2_src.at[slot_rows(v)], c2_dst.at[slot_rows(me)], c2_s, c2_r, device)
+
+    def c2_all():
+        at = pl.ds(0, (units - 1) * capacity)
+        return remote(c2_src.at[at], c2_dst.at[at], c2_s, c2_r, peer)
 
     def c2_send():
         total = y[image_rows, my_cols]
+        c1_all(image_rows, ci_s, ci_r).wait_recv()
         for i in range(1, tp):
             q = head_of(i)[0]
-            c1(i, q, image_rows, ci_s, ci_r).wait_recv()
             total = total + yr[q, image_rows, :].astype(f32)
         c2_src[...] = jnp.dot(pick_t[...], total.astype(bf16), preferred_element_type=f32).astype(bf16)
         for i in range(1, units):
             c2(i).start()
         c2_dst[slot_rows(me), :] = c2_src[slot_rows(me), :]
 
-    def g_slice(b, c):
-        return pl.ds(pl.multiple_of(b * block + c * g_rows, g_rows), g_rows)
+    def home(b, c):
+        return jnp.where(c < G_MAIN, z0, other_z0) + b
 
     def chain_copies(b, c):
         i, at = b * G_PARTS + c, g_slice(b, c)
         return (
-            (z > z0 + b, remote(chain.at[at], above.at[at], ch_s.at[i], ab_r.at[i], (g, z - 1, t))),
-            (z < z0 + b, remote(chain.at[at], below.at[at], ch_s.at[i], be_r.at[i], (g, z + 1, t))),
+            (z > home(b, c), remote(chain.at[at], above.at[at], ch_s, ab_r.at[i], (g, z - 1, t))),
+            (z < home(b, c), remote(chain.at[at], below.at[at], ch_s, be_r.at[i], (g, z + 1, t))),
         )
 
     def landing(c):
@@ -531,23 +646,36 @@
 
     def result_copy(b, c, q):
         return remote(
-            chain.at[g_slice(b, c), q * cols : (q + 1) * cols], landing(c), g_s.at[c * tp + q], g_r.at[c], (1 - g, z, q)
+            chain.at[g_slice(b, c), q * cols : (q + 1) * cols], landing(c), g_s, g_r, (1 - g, z, q)
         )
 
     def g_step(m):
-        b, c = near_block(blocks - 1 - m // G_PARTS), lax.rem(m, G_PARTS)
-        i, at, zb = b * G_PARTS + c, g_slice(b, c), z0 + b
-        p_copy(i).wait_recv()
-        pf[at, :] += pb[at, :].astype(f32)
+        sides = blocks * (G_PARTS - G_MAIN)
+        mains = blocks * G_MAIN
+        own = jnp.where(inside, m >= sides, m < mains)
+        own_m, other_m = jnp.where(inside, m - sides, m), jnp.where(inside, m, m - mains)
+        b = jnp.where(own, near_block(blocks - 1 - own_m // G_MAIN), far_other(other_m // (G_PARTS - G_MAIN)))
+        c = jnp.where(own, lax.rem(own_m, G_MAIN), G_MAIN + lax.rem(other_m, G_PARTS - G_MAIN))
+        i, at, zb = b * G_PARTS + c, g_slice(b, c), home(b, c)
+
+        @pl.when(own)
+        def _():
+            p_copy(i).wait_recv()
+            pf[at, :] += pb[at, :].astype(f32)
+
+        @pl.when(jnp.logical_not(own))
+        def _():
+            x_copy(b, c).wait_recv()
+            pf[at, :] = pa[at, :].astype(f32)
 
         @pl.when((z >= zb) & (z < fsdp - 1))
         def _():
-            remote(chain.at[at], above.at[at], ch_s.at[i], ab_r.at[i], peer).wait_recv()
+            remote(chain.at[at], above.at[at], ch_s, ab_r.at[i], peer).wait_recv()
             pf[at, :] += above[at, :].astype(f32)
 
         @pl.when((z <= zb) & (z > 0))
         def _():
-            remote(chain.at[at], below.at[at], ch_s.at[i], be_r.at[i], peer).wait_recv()
+            remote(chain.at[at], below.at[at], ch_s, be_r.at[i], peer).wait_recv()
             pf[at, :] += below[at, :].astype(f32)
 
         chain[at, :] = pf[at, :].astype(bf16)
@@ -560,14 +688,22 @@
                 result_copy(b, c, q).start()
 
     ratio = g_steps // w_steps
-    turns = 2 * w_steps
+    half = w_steps // 2
+    lead = blocks * G_MAIN // ratio
+    turns = w_steps + lead + 1
     sums = jnp.logical_not(carries)
-    w_at = jnp.where(sums & far_end, w_steps, 0)
-    g_at = jnp.where(far_end, 0, jnp.where(inside, w_steps, w_steps // 2 - 1))
-    c2_at = jnp.where(sums & inside, w_steps + w_steps // 2, jnp.where(sums & jnp.logical_not(far_end), w_steps + 1, turns - 1))
+    late = sums & far_end
+    w_at = jnp.where(late, lead, 0)
+    c2_at = jnp.where(carries, w_steps - 1, jnp.where(far_end, lead + w_steps - 1, w_steps + 1))
 
     def turn(s, carry):
-        n, m = s - w_at, s - g_at
+        n = s - w_at
+        late_m = jnp.where(s < lead, s, jnp.where(s == lead + w_steps - 2, lead, jnp.where(s == lead + w_steps, lead + 1, -1)))
+        m = jnp.where(late, late_m, s - 3)
+
+        @pl.when(carries & inside & jnp.logical_not(entry) & (s == half))
+        def _():
+            side_forward(side_block(1))
 
         @pl.when(sums & (m >= 0) & (m < w_steps))
         def _():
@@ -585,14 +721,39 @@
 
     lax.fori_loop(0, turns, turn, 0)
 
+    def each(count, body):
+        lax.fori_loop(0, count, lambda n, unused: (body(n), unused)[1], 0)
+
+    def w_sent(n):
+        b, c = n // W_PARTS, lax.rem(n, W_PARTS)
+        for condition, copy in w_routes(b, c):
+            pl.when(condition)(copy.wait_send)
+
+    def side_sent(b):
+        passes = inside | (z == other_z0 + b) | (border & (b == side_block(1)))
+        for condition, copy in side_routes(b):
+            pl.when(condition & passes)(copy.wait_send)
+
+    @pl.when(carries)
+    def _():
+        each(w_steps, w_sent)
+        each(blocks, side_sent)
+        remote(w, w, w_dd, w_dd, peer).wait_send()
+        remote(pa, pb, p_s, p_s, peer).wait_send()
+
+    @pl.when(sums)
+    def _():
+        at = pl.ds(0, blocks * (G_PARTS - G_MAIN) * g_rows)
+        remote(pb.at[at], pa.at[at], x_s, x_s, beside).wait_send()
+
+    d1_all().wait_send()
+    d2_all().wait_send()
+    c1_all(image_rows, ci_s, ci_r).wait_send()
     total = y[text_rows, my_cols]
+    c1_all(text_rows, ct_s, ct_r).wait_recv()
     for i in range(1, tp):
-        q = head_of(i)[0]
-        c1(i, q, text_rows, ct_s, ct_r).wait_recv()
-        total = total + yr[q, text_rows, :].astype(f32)
-    for i in range(1, units):
-        v, device = unit_of(i)
-        remote(c2_src.at[slot_rows(v)], c2_dst.at[slot_rows(v)], c2_s.at[v], c2_r.at[v], device).wait_recv()
+        total = total + yr[head_of(i)[0], text_rows, :].astype(f32)
+    c2_all().wait_recv()
     placed = lax.dot_general(place_t[...], c2_dst[...], ROWS_TO_COLS, preferred_element_type=f32)
     projected = jnp.where(is_img[...] > 0.5, placed, total) + bias_ref[...]
     for s in range(rows // LENGTH):
@@ -600,45 +761,19 @@
         turned = values * cosv[...] + pltpu.roll(values, HALF, 1) * sinv[...]
         keys_out[s * LENGTH : (s + 1) * LENGTH, :] = jnp.where(live(s), turned, 0.0).astype(bf16)
 
-    for c in range(G_PARTS):
-        remote(landing(c), landing(c), g_s.at[0], g_r.at[c], peer).wait_recv()
+    remote(landed, landed, g_s, g_r, peer).wait_recv()
     wgrad_out[...] = landed[...].astype(f32) * (1.0 / rows)
 
-    def each(count, body):
-        lax.fori_loop(0, count, lambda n, unused: (body(n), unused)[1], 0)
-
-    def w_sent(n):
-        b, c = n // W_PARTS, lax.rem(n, W_PARTS)
-        for condition, copy in w_routes(b, c):
-            pl.when(condition)(copy.wait_send)
-        w_send(b, c, peer, w_dd).wait_send()
-
-    @pl.when(carries)
-    def _():
-        each(w_steps, w_sent)
-        each(g_steps, lambda n: p_copy(n).wait_send())
-
-    def g_sent(n):
-        b, c = n // G_PARTS, lax.rem(n, G_PARTS)
-        for condition, copy in chain_copies(b, c):
-            pl.when(condition)(copy.wait_send)
-
-        @pl.when(z == z0 + b)
-        def _():
-            for q in range(tp):
-                result_copy(b, c, q).wait_send()
-
-    @pl.when(sums)
-    def _():
-        each(g_steps, g_sent)
-
-    for i in range(1, units):
-        d1(i).wait_send()
-        c2(i).wait_send()
-    for i in range(1, tp):
-        d2(i, t).wait_send()
-        c1(i, t, image_rows, ci_s, ci_r).wait_send()
-        c1(i, t, text_rows, ct_s, ct_r).wait_send()
+    for condition, parts in ((inside, G_MAIN), (jnp.logical_not(inside), G_PARTS - G_MAIN)):
+
+        @pl.when(sums & condition)
+        def _():
+            ends, passed = pl.ds(0, parts * g_rows), pl.ds(0, (g_steps - parts) * g_rows)
+            remote(chain.at[ends], above.at[ends], g_s, g_s, peer).wait_send()
+            remote(chain.at[passed], above.at[passed], ch_s, ch_s, peer).wait_send()
+
+    c1_all(text_rows, ct_s, ct_r).wait_send()
+    c2_all().wait_send()
 
 
 def write_kernel(*refs):
@@ -665,7 +800,7 @@
     if groups != 2 or units % tp or head_cols != HEAD_DIM or rows % LENGTH:
         return False
     blocks = units // tp
-    return blocks == 2 and fsdp % blocks == 0 and block % (G_PARTS * HEAD_DIM) == 0 and (rows // units) % 16 == 0
+    return blocks == 2 and fsdp == 2 * blocks and tp % 2 == 0 and block % (G_PARTS * HEAD_DIM) == 0 and (rows // units) % 16 == 0
 
 
 def per_device(
@@ -691,6 +826,7 @@
     hbm = pl.BlockSpec(memory_space=pltpu.HBM)
     vmem = pl.BlockSpec(memory_space=pltpu.VMEM)
     dma = lambda n: pltpu.SemaphoreType.DMA((n,))
+    one = pltpu.SemaphoreType.DMA
     shapes = (
         jax.ShapeDtypeStruct((rows, cols), bf16),
         jax.ShapeDtypeStruct((rows, columns), bf16),
@@ -735,11 +871,11 @@
             pltpu.VMEM((slots, cols), bf16),
             pltpu.VMEM((slots, cols), bf16),
             pltpu.VMEM((block, cols), bf16),
-            dma(9), dma(w_steps), dma(w_steps), dma(w_steps), dma(w_steps),
-            dma(units), dma(units), dma(tp), dma(tp),
-            dma(tp), dma(tp), dma(tp), dma(tp), dma(units), dma(units),
-            dma(g_steps), dma(g_steps), dma(g_steps), dma(g_steps), dma(g_steps),
-            dma(G_PARTS * tp), dma(G_PARTS),
+            pltpu.VMEM((blocks, block // W_PARTS, key_cols), bf16),
+            dma(9), dma(w_steps), dma(w_steps), dma(w_steps), one,
+            one, one, one, one, one, one, one, one, one, one,
+            one, dma(g_steps), dma(g_steps), dma(g_steps), one, one, one,
+            one, dma(g_steps), dma(blocks), dma(blocks), dma(blocks),
         ],
         compiler_params=pltpu.CompilerParams(
             collective_id=0, has_side_effects=True, vmem_limit_bytes=44 * 1024 * 1024

time: 56.4 us -> 50.3 us (0.89); the launches traced: 55.5 us -> 50.1 us
  Pallas kernels: 54.9 us -> 49.5 us
    pallas_call x1, Pallas kernels: 53 us -> 47.6 us  [per_device(): pl.pallas_call(functools.partial(fused_kernel, groups, fsdp, tp, capacity...]
where the time goes in v3:
time: 50.3 us; the launch traced here: 50.1 us
  Pallas kernels  49.5 us (98%)
  between operations  0.64 us (1%)
    pallas_call x1, Pallas kernels, per_device(): pl.pallas_call(functools.partial(fused_kernel, groups, fsdp, tp, capacity...  47.6 us
    pallas_call x1, Pallas kernels, per_device(): pl.pallas_call(write_kernel, out_shape=shapes, in_specs=[vmem] * 4, out_s...  1.91 us

profile of v3, /device:TPU:0, one launch (start us, length us, event | category | flops | bytes accessed | tf_op | source)
XLA Modules:
  0.0 50.1 jit_solution(13912468340482766741)
XLA Ops:
  0.6 47.6 %fused.1 = (bf16[512,128]{1,0:T(8,128)(2,1)S(1)}, bf16[512,2048]{1,0:T(8,128)(2,1)S(1)}, bf16[256,2048]{1,0:T(8,128)(2,1)S(1)}, f32[1024,128]{1,0:T(8,128)S(1)}) custom-call(bf16[512,2048]{1,0:T(8,128)(2,1)} %text_ref.1, bf16[256,2048]{1,0:T(8,128)(2,1)} %image_ref.1, bf16[1024,512]{1,0:T(8,128)(2,1)} %weight_ref.1, f32[1,128]{1,0:T(1,128)} %bitcast.6, ...), custom_call_target="tpu_custom_call" | custom-call | tf_op jit(solution)/shard_map/fused/pallas_call | solution.py:840
  48.2 1.9 %write.1 = (bf16[512,128]{1,0:T(8,128)(2,1)}, bf16[512,2048]{1,0:T(8,128)(2,1)}, bf16[256,2048]{1,0:T(8,128)(2,1)}, f32[1024,128]{1,0:T(8,128)}) custom-call(bf16[512,128]{1,0:T(8,128)(2,1)S(1)} %get-tuple-element.8.refs_0_, bf16[512,2048]{1,0:T(8,128)(2,1)S(1)} %get-tuple-element.9.refs_1_, bf16[256,2048]{1,0:T(8,128)(2,1)S(1)} %get-tuple-element.10.refs_2_, ...), custom_call_target="tpu_custom_call" | custom-call | tf_op jit(solution)/shard_map/write/pallas_call | solution.py:885

commit v4 on v3

--- a/solution.py
+++ b/solution.py
@@ -244,8 +244,15 @@
 COLS_TO_COLS = (((1,), (1,)), ((), ()))
 W_PARTS = 4
 W_MAIN = 3
+W_FINE = 2
+W_NEAR_OR_FAR = (0, 0, 0, 1, 0, 1, 1, 1)
+W_PART_AT = (0, 1, 2, 0, 3, 1, 3, 2)
+FAR_STEPS = (0, 2, 4, 6, 8, 10, 10, 10, 10, 10, 13, 13, 13, 13, 16)
+BORDER_STEPS = (0, 0, 0, 0, 2, 4, 6, 8, 8, 13, 13, 16, 16, 16, 16)
+ENTRY_STEPS = (0, 0, 0, 0, 0, 0, 0, 0, 0, 4, 8, 14, 16, 16, 16)
+LAST_STEPS = (0, 0, 0, 0, 2, 4, 6, 9, 11, 13, 13, 16, 16, 16, 16)
 G_PARTS = 8
-G_MAIN = 6
+G_MAIN = 5
 
 
 def fused_kernel(
@@ -254,8 +261,7 @@
     keys_out, text_out, image_out, wgrad_out,
     bias_ref, owner_ref, slot_ref, lens_ref, x, w, cot, cosv, sinv, back, pick_t, place_t, is_img,
     d1_src, d1_dst, d2_src, pf, pa, pb, chain, above, below, y, yb, yr, c2_src, c2_dst, landed, side,
-    ld, w_recv, w_up, w_dn, w_dd, d1_s, d1_r, d2_s, d2_r, ci_s, ci_r, ct_s, ct_r, c2_s, c2_r,
-    p_s, p_r, ab_r, be_r, ch_s, g_s, g_r, x_s, x_r, h_r, h_z, h_x,
+    ld, w_recv, sent, shared, small, d1_r, d2_r, ci_r, ct_r, c2_r, g_r, p_r, chain_r, x_r, h_r,
 ):
     f32, bf16 = jnp.float32, jnp.bfloat16
     g, z, t = lax.axis_index("group"), lax.axis_index("fsdp"), lax.axis_index("tp")
@@ -268,6 +274,7 @@
     cols = bias_ref.shape[1]
     block = weight_ref.shape[0]
     blocks = units // tp
+    key_cols = tp * cols
     w_rows, g_rows = block // W_PARTS, block // G_PARTS
     w_steps, g_steps = blocks * W_PARTS, blocks * G_PARTS
     first = t * blocks
@@ -275,7 +282,6 @@
     carries = g == carrier
     inside = (z >= z0) & (z < z0 + blocks)
     far_end = jnp.logical_not(inside) & ((z == 0) | (z == fsdp - 1))
-    adjacent = inside | (z == z0 - 1) | (z == z0 + blocks)
     my_cols = pl.ds(pl.multiple_of(t * cols, cols), cols)
     peer = (1 - g, z, t)
     other = lax.bitwise_xor(t, 1)
@@ -284,6 +290,7 @@
     upward = z0 > 0
     entry = jnp.where(upward, z == z0, z == z0 + blocks - 1)
     border = jnp.where(upward, z == z0 - 1, z == z0 + blocks)
+    relays = entry | border
 
     def near_block(k):
         within = lax.rem(z - z0 + k + blocks, blocks)
@@ -293,10 +300,14 @@
         within = lax.rem(z - other_z0 + blocks - 1 - k + blocks, blocks)
         return jnp.where(inside, jnp.where(upward, k, blocks - 1 - k), within)
 
+    def look_up(table, n):
+        found = table[0]
+        for i in range(1, len(table)):
+            found = jnp.where(n == i, table[i], found)
+        return found
+
     def w_part(n):
-        late = n >= blocks * W_MAIN
-        k = jnp.where(late, n - blocks * W_MAIN, n // W_MAIN)
-        return near_block(k), jnp.where(late, W_MAIN, lax.rem(n, W_MAIN))
+        return near_block(look_up(W_NEAR_OR_FAR, n)), look_up(W_PART_AT, n)
 
     def unit_of(i):
         v = lax.rem(me + i, units)
@@ -337,22 +348,35 @@
     def w_slice(b, c):
         return pl.ds(pl.multiple_of(b * block + c * w_rows, w_rows), w_rows)
 
-    def w_load(b, c):
-        return pltpu.make_async_copy(
-            weight_ref.at[pl.ds(pl.multiple_of(c * w_rows, w_rows), w_rows)], w.at[w_slice(b, c)], w_recv.at[b * W_PARTS + c]
-        )
+    fine = w_rows // W_FINE
+
+    def w_fine(b, c, h):
+        return pl.ds(pl.multiple_of(b * block + c * w_rows + h * fine, fine), fine)
+
+    def w_index(b, c, h):
+        return (b * W_PARTS + c) * W_FINE + h
+
+    def w_load(b, c, h):
+        source = weight_ref.at[pl.ds(pl.multiple_of(c * w_rows + h * fine, fine), fine)]
+        return pltpu.make_async_copy(source, w.at[w_fine(b, c, h)], w_recv.at[w_index(b, c, h)])
+
+    def side_rows(b, h):
+        return side.at[b, pl.ds(h * fine, fine)]
+
+    def side_load(b, h):
+        source = weight_ref.at[pl.ds(W_MAIN * w_rows + h * fine, fine)]
+        return pltpu.make_async_copy(source, side_rows(b, h), h_r.at[b * W_FINE + h])
 
     @pl.when(carries & inside)
     def _():
         for c in range(W_PARTS):
-            w_load(z - z0, c).start()
-
-    def side_load(b):
-        return pltpu.make_async_copy(weight_ref.at[pl.ds(W_MAIN * w_rows, w_rows)], side.at[b], h_r.at[b])
+            for h in range(W_FINE):
+                w_load(z - z0, c, h).start()
 
     @pl.when(carries & jnp.logical_not(inside))
     def _():
-        side_load(z - other_z0).start()
+        for h in range(W_FINE):
+            side_load(z - other_z0, h).start()
 
     for load in loads[5:]:
         load.start()
@@ -385,58 +409,59 @@
 
     def d1(i):
         v, device = unit_of(i)
-        return remote(d1_src.at[slot_rows(v)], d1_dst.at[slot_rows(me)], d1_s, d1_r, device)
+        return remote(d1_src.at[slot_rows(v)], d1_dst.at[slot_rows(me)], small, d1_r, device)
 
     def d1_all():
         at = pl.ds(0, (units - 1) * capacity)
-        return remote(d1_src.at[at], d1_dst.at[at], d1_s, d1_r, peer)
+        return remote(d1_src.at[at], d1_dst.at[at], small, d1_r, peer)
 
     for i in range(1, units):
         d1(i).start()
     d1_dst[slot_rows(me), :] = d1_src[slot_rows(me), :]
 
-    def w_send(b, c, to, sem):
-        i = b * W_PARTS + c
-        return remote(w.at[w_slice(b, c)], w.at[w_slice(b, c)], sem.at[i], w_recv.at[i], to)
-
-    def w_share(b, c):
-        return remote(w.at[w_slice(b, c)], w.at[w_slice(b, c)], w_dd, w_recv.at[b * W_PARTS + c], peer)
-
-    def w_routes(b, c):
-        return (
-            ((z >= z0 + b) & (z < fsdp - 1) & ((c < W_MAIN) | (z + 1 < z0 + blocks)), w_send(b, c, (g, z + 1, t), w_up)),
-            ((z <= z0 + b) & (z > 0) & ((c < W_MAIN) | (z > z0)), w_send(b, c, (g, z - 1, t), w_dn)),
-        )
+    def w_send(b, c, h, to):
+        at = w_fine(b, c, h)
+        return remote(w.at[at], w.at[at], sent, w_recv.at[w_index(b, c, h)], to)
+
+    def w_share(b, c, h):
+        at = w_fine(b, c, h)
+        return remote(w.at[at], w.at[at], shared, w_recv.at[w_index(b, c, h)], peer)
+
+    def w_routes(b, c, h):
+        up = (z >= z0 + b) & (z < fsdp - 1) & ((c < W_MAIN) | (z + 1 < z0 + blocks))
+        down = (z <= z0 + b) & (z > 0) & ((c < W_MAIN) | (z > z0))
+        return ((up, w_send(b, c, h, (g, z + 1, t))), (down, w_send(b, c, h, (g, z - 1, t))))
 
     def w_inward(c):
         b = z - z0
+        for h in range(W_FINE):
+            pl.when(upward)(w_send(b, c, h, (g, z + 1, t)).start)
+            pl.when(jnp.logical_not(upward))(w_send(b, c, h, (g, z - 1, t)).start)
+
+    def side_routes(b, h):
+        step = jnp.where(upward, 1, -1)
+        i, at = b * W_FINE + h, w_fine(b, W_MAIN, h)
         return (
-            (upward, w_send(b, c, (g, z + 1, t), w_up)),
-            (jnp.logical_not(upward), w_send(b, c, (g, z - 1, t), w_dn)),
+            ((z + step >= 0) & (z + step < fsdp), remote(side_rows(b, h), side_rows(b, h), sent, h_r.at[i], (g, z + step, t))),
+            (inside, remote(side_rows(b, h), w.at[at], sent, w_recv.at[w_index(b, W_MAIN, h)], beside)),
         )
 
-    def side_routes(b):
-        step = jnp.where(upward, 1, -1)
-        at = w_slice(b, W_MAIN)
-        return (
-            ((z + step >= 0) & (z + step < fsdp), remote(side.at[b], side.at[b], h_z.at[b], h_r.at[b], (g, z + step, t))),
-            (inside, remote(side.at[b], w.at[at], h_x.at[b], w_recv.at[b * W_PARTS + W_MAIN], beside)),
-        )
-
     def side_forward(b):
-        side_load(b).wait()
-        for condition, copy in side_routes(b):
-            pl.when(condition)(copy.start)
+        for h in range(W_FINE):
+            side_load(b, h).wait()
+            for condition, copy in side_routes(b, h):
+                pl.when(condition)(copy.start)
 
     def side_block(k):
         return jnp.where(upward, blocks - 1 - k, k)
 
     def w_forward(b, c):
-        w_load(b, c).wait()
         held = entry & (z == z0 + b) & (c >= 2)
-        for (condition, copy), inward in zip(w_routes(b, c), (upward, jnp.logical_not(upward))):
-            pl.when(condition & jnp.logical_not(held & inward))(copy.start)
-        w_share(b, c).start()
+        for h in range(W_FINE):
+            w_load(b, c, h).wait()
+            for (condition, copy), inward in zip(w_routes(b, c, h), (upward, jnp.logical_not(upward))):
+                pl.when(condition & jnp.logical_not(held & inward))(copy.start)
+            w_share(b, c, h).start()
 
     @pl.when(carries & inside)
     def _():
@@ -446,7 +471,7 @@
     def _():
         side_forward(z - other_z0)
 
-    base = jnp.where(inside, W_MAIN, 0)
+    early = jnp.where(inside, near_block(1), near_block(0))
 
     y[...] = jnp.zeros_like(y)
     for s in range(rows // LENGTH):
@@ -491,22 +516,22 @@
 
     def d2(i, source):
         q, device = head_of(i)
-        return remote(d2_src, back.at[pl.ds(rows, images), head_cols(source)], d2_s, d2_r, device)
+        return remote(d2_src, back.at[pl.ds(rows, images), head_cols(source)], small, d2_r, device)
 
     text_rows, image_rows = pl.ds(0, rows), pl.ds(rows, images)
 
     def d2_all():
         at = pl.ds(0, tp - 1)
-        return remote(yb.at[at, image_rows], yr.at[at, image_rows], d2_s, d2_r, peer)
+        return remote(yb.at[at, image_rows], yr.at[at, image_rows], small, d2_r, peer)
 
     for i in range(1, tp):
         d2(i, t).start()
 
-    @pl.when(carries & adjacent)
-    def _():
-        w_forward(*w_part(base))
-
-    @pl.when(carries & (border | entry))
+    @pl.when(carries & (inside | border))
+    def _():
+        w_forward(early, 0)
+
+    @pl.when(carries & relays)
     def _():
         side_forward(side_block(jnp.where(border, 1, 0)))
 
@@ -514,26 +539,20 @@
     loads[6].wait()
     loads[8].wait()
 
-    @pl.when(carries & adjacent)
-    def _():
-        w_forward(*w_part(base + 1))
-
-    @pl.when(carries & entry)
-    def _():
-        for c in range(2, W_PARTS):
-            for condition, copy in w_inward(c):
-                pl.when(condition)(copy.start)
+    @pl.when(carries & (inside | border))
+    def _():
+        w_forward(early, 1)
 
     def p_copy(i):
         at = pl.ds(pl.multiple_of(i * g_rows, g_rows), g_rows)
-        return remote(pa.at[at], pb.at[at], p_s, p_r.at[i], peer)
+        return remote(pa.at[at], pb.at[at], shared, p_r.at[i], peer)
 
     def g_slice(b, c):
         return pl.ds(pl.multiple_of(b * block + c * g_rows, g_rows), g_rows)
 
     def x_copy(b, c):
-        i, at = b * G_PARTS + c, g_slice(b, c)
-        return remote(pb.at[at], pa.at[at], x_s, x_r.at[i], beside)
+        i, at = b * (G_PARTS - G_MAIN) + c - G_MAIN, g_slice(b, c)
+        return remote(pb.at[at], pa.at[at], sent, x_r.at[i], beside)
 
     def x_send(b, c):
         i, at = b * G_PARTS + c, g_slice(b, c)
@@ -542,7 +561,7 @@
         x_copy(b, c).start()
 
     def p_step(k, carry):
-        b, half = near_block(blocks - 1 - k // 2), 1 - lax.rem(k, 2)
+        b, half = near_block(blocks - 1 - k // 2), lax.rem(k, 2)
         j = b * 2 + half
         at = pl.ds(pl.multiple_of(j * tile, tile), tile)
         part = pf[at, :] + lax.dot_general(
@@ -556,27 +575,29 @@
             for c in range(tile // g_rows):
                 p_copy(j * (tile // g_rows) + c).start()
 
-        @pl.when(jnp.logical_not(carries) & (half == 0))
-        def _():
-            lax.fori_loop(G_MAIN, G_PARTS, lambda c, unused: (x_send(b, c), unused)[1], 0)
-
         return carry
 
     lax.fori_loop(0, columns // tile, p_step, 0)
 
-    @pl.when(carries & adjacent)
-    def _():
-        w_forward(*w_part(base + 2))
+    @pl.when(carries & relays)
+    def _():
+        w_forward(early, 2)
 
     @pl.when(carries & inside)
     def _():
         side_forward(side_block(jnp.where(entry, 1, 0)))
+
+    @pl.when(carries & entry)
+    def _():
+        for c in range(2, W_PARTS):
+            w_inward(c)
 
     def w_step(n):
         b, c = w_part(n)
         ahead = jnp.where(border, n + 3, n)
         next_b, next_c = w_part(ahead)
-        forwarded = (adjacent & (ahead >= base) & (ahead < base + 3)) | (inside & (z == z0 + next_b))
+        main = next_c < W_MAIN
+        forwarded = (inside & (z == z0 + next_b)) | ((relays & main | inside & (next_c < 2)) & (next_b == early))
 
         @pl.when(carries & (ahead < w_steps) & jnp.logical_not(forwarded))
         def _():
@@ -584,45 +605,53 @@
 
         @pl.when(jnp.logical_not(carries))
         def _():
-            w_load(b, c).wait()
+            for h in range(W_FINE):
+                w_load(b, c, h).wait()
 
         at = w_slice(b, c)
-        for which, send, recv in ((image_rows, ci_s, ci_r), (text_rows, ct_s, ct_r)):
+        for which, recv in ((image_rows, ci_r), (text_rows, ct_r)):
             y[which, :] += jnp.dot(x[which, at], w[at, :], preferred_element_type=f32)
 
             @pl.when(n == w_steps - 1)
             def _():
-                c1_send(which, send, recv)
-
+                c1_send(which, recv)
+
+        last, kept = n == w_steps - 1, w_steps - 3
+        start = jnp.where(last, kept, n)
+        lax.fori_loop(start, jnp.where((n < kept) | last, n + 1, n), grad_step, 0)
+
+    def grad_step(n, carry):
+        at = w_slice(*w_part(n))
         grads = lax.dot_general(back[...], w[at, :], COLS_TO_COLS, preferred_element_type=f32).astype(bf16)
         text_out[:, at] = grads[:rows]
         image_out[:, at] = grads[rows:]
-
-    def c1(i, source, which, send, recv):
+        return carry
+
+    def c1(i, source, which, recv):
         q, device = head_of(i)
-        return remote(yb.at[q, which], yr.at[source, which], send, recv, device)
-
-    def c1_all(which, send, recv):
+        return remote(yb.at[q, which], yr.at[source, which], small, recv, device)
+
+    def c1_all(which, recv):
         at = pl.ds(0, tp - 1)
-        return remote(yb.at[at, which], yr.at[at, which], send, recv, peer)
-
-    def c1_send(which, send, recv):
+        return remote(yb.at[at, which], yr.at[at, which], small, recv, peer)
+
+    def c1_send(which, recv):
         for q in range(tp):
             yb[q, which, :] = y[which, q * cols : (q + 1) * cols].astype(bf16)
         for i in range(1, tp):
-            c1(i, t, which, send, recv).start()
+            c1(i, t, which, recv).start()
 
     def c2(i):
         v, device = unit_of(i)
-        return remote(c2_src.at[slot_rows(v)], c2_dst.at[slot_rows(me)], c2_s, c2_r, device)
+        return remote(c2_src.at[slot_rows(v)], c2_dst.at[slot_rows(me)], small, c2_r, device)
 
     def c2_all():
         at = pl.ds(0, (units - 1) * capacity)
-        return remote(c2_src.at[at], c2_dst.at[at], c2_s, c2_r, peer)
+        return remote(c2_src.at[at], c2_dst.at[at], small, c2_r, peer)
 
     def c2_send():
         total = y[image_rows, my_cols]
-        c1_all(image_rows, ci_s, ci_r).wait_recv()
+        c1_all(image_rows, ci_r).wait_recv()
         for i in range(1, tp):
             q = head_of(i)[0]
             total = total + yr[q, image_rows, :].astype(f32)
@@ -637,8 +666,8 @@
     def chain_copies(b, c):
         i, at = b * G_PARTS + c, g_slice(b, c)
         return (
-            (z > home(b, c), remote(chain.at[at], above.at[at], ch_s, ab_r.at[i], (g, z - 1, t))),
-            (z < home(b, c), remote(chain.at[at], below.at[at], ch_s, be_r.at[i], (g, z + 1, t))),
+            (z > home(b, c), remote(chain.at[at], above.at[at], sent, chain_r.at[i], (g, z - 1, t))),
+            (z < home(b, c), remote(chain.at[at], below.at[at], sent, chain_r.at[i], (g, z + 1, t))),
         )
 
     def landing(c):
@@ -646,14 +675,13 @@
 
     def result_copy(b, c, q):
         return remote(
-            chain.at[g_slice(b, c), q * cols : (q + 1) * cols], landing(c), g_s, g_r, (1 - g, z, q)
+            chain.at[g_slice(b, c), q * cols : (q + 1) * cols], landing(c), sent, g_r, (1 - g, z, q)
         )
 
     def g_step(m):
-        sides = blocks * (G_PARTS - G_MAIN)
-        mains = blocks * G_MAIN
-        own = jnp.where(inside, m >= sides, m < mains)
-        own_m, other_m = jnp.where(inside, m - sides, m), jnp.where(inside, m, m - mains)
+        own = jnp.where(inside, m >= blocks * (G_PARTS - G_MAIN), m < blocks * G_MAIN)
+        own_m = jnp.where(inside, m - blocks * (G_PARTS - G_MAIN), m)
+        other_m = jnp.where(inside, m, m - blocks * G_MAIN)
         b = jnp.where(own, near_block(blocks - 1 - own_m // G_MAIN), far_other(other_m // (G_PARTS - G_MAIN)))
         c = jnp.where(own, lax.rem(own_m, G_MAIN), G_MAIN + lax.rem(other_m, G_PARTS - G_MAIN))
         i, at, zb = b * G_PARTS + c, g_slice(b, c), home(b, c)
@@ -668,15 +696,22 @@
             x_copy(b, c).wait_recv()
             pf[at, :] = pa[at, :].astype(f32)
 
-        @pl.when((z >= zb) & (z < fsdp - 1))
-        def _():
-            remote(chain.at[at], above.at[at], ch_s, ab_r.at[i], peer).wait_recv()
-            pf[at, :] += above[at, :].astype(f32)
-
-        @pl.when((z <= zb) & (z > 0))
-        def _():
-            remote(chain.at[at], below.at[at], ch_s, be_r.at[i], peer).wait_recv()
-            pf[at, :] += below[at, :].astype(f32)
+        from_above, from_below = (z >= zb) & (z < fsdp - 1), (z <= zb) & (z > 0)
+        pair = pl.ds(0, 2 * g_rows)
+
+        @pl.when(from_above & from_below)
+        def _():
+            remote(chain.at[pair], above.at[pair], sent, chain_r.at[i], peer).wait_recv()
+
+        @pl.when(from_above != from_below)
+        def _():
+            remote(chain.at[at], above.at[at], sent, chain_r.at[i], peer).wait_recv()
+
+        for arrives, source in ((from_above, above), (from_below, below)):
+
+            @pl.when(arrives)
+            def _():
+                pf[at, :] += source[at, :].astype(f32)
 
         chain[at, :] = pf[at, :].astype(bf16)
         for condition, copy in chain_copies(b, c):
@@ -689,25 +724,43 @@
 
     ratio = g_steps // w_steps
     half = w_steps // 2
-    lead = blocks * G_MAIN // ratio
-    turns = w_steps + lead + 1
+    mains, sides = blocks * G_MAIN, G_PARTS - G_MAIN
+    lead = mains // ratio
+    turns = len(FAR_STEPS) - 1
     sums = jnp.logical_not(carries)
     late = sums & far_end
     w_at = jnp.where(late, lead, 0)
-    c2_at = jnp.where(carries, w_steps - 1, jnp.where(far_end, lead + w_steps - 1, w_steps + 1))
+    c2_at = jnp.where(far_end, lead + w_steps - 1, jnp.where(entry, w_steps + 2, w_steps + 1))
+    c2_at = jnp.where(carries, w_steps - 1, c2_at)
+    spot = mains - ratio
+
+    def in_turn(m):
+        moved = jnp.where(m < spot + sides, m - spot + mains, jnp.where(m < mains + sides, m - sides, m))
+        group, place = m // (2 * ratio), lax.rem(m, 2 * ratio)
+        woven = jnp.where(place < ratio, blocks * sides, -ratio) + group * ratio + place
+        woven = jnp.where(m < 2 * blocks * sides, woven, m)
+        return jnp.where(border & (m >= spot), moved, jnp.where(entry, woven, m))
 
     def turn(s, carry):
         n = s - w_at
-        late_m = jnp.where(s < lead, s, jnp.where(s == lead + w_steps - 2, lead, jnp.where(s == lead + w_steps, lead + 1, -1)))
-        m = jnp.where(late, late_m, s - 3)
+        done = look_up(FAR_STEPS, s), look_up(FAR_STEPS, s + 1)
+        for kind, steps in ((border, BORDER_STEPS), (entry, ENTRY_STEPS), (inside & jnp.logical_not(entry), LAST_STEPS)):
+            done = tuple(jnp.where(kind, look_up(steps, s + i), done[i]) for i in range(2))
+        g_lo, g_hi = done
+
+        x_at = jnp.where(late, jnp.where(s == 1, 0, jnp.where(s == lead // 2 + 1, 1, -1)), jnp.where(s < blocks, s, -1))
 
         @pl.when(carries & inside & jnp.logical_not(entry) & (s == half))
         def _():
             side_forward(side_block(1))
 
-        @pl.when(sums & (m >= 0) & (m < w_steps))
-        def _():
-            lax.fori_loop(0, ratio, lambda k, unused: (g_step(m * ratio + k), unused)[1], 0)
+        @pl.when(sums)
+        def _():
+            lax.fori_loop(g_lo, g_hi, lambda m, unused: (g_step(in_turn(m)), unused)[1], 0)
+
+        @pl.when(sums & (x_at >= 0))
+        def _():
+            lax.fori_loop(G_MAIN, G_PARTS, lambda c, unused: (x_send(near_block(blocks - 1 - x_at), c), unused)[1], 0)
 
         @pl.when((n >= 0) & (n < w_steps))
         def _():
@@ -721,36 +774,24 @@
 
     lax.fori_loop(0, turns, turn, 0)
 
-    def each(count, body):
-        lax.fori_loop(0, count, lambda n, unused: (body(n), unused)[1], 0)
-
-    def w_sent(n):
-        b, c = n // W_PARTS, lax.rem(n, W_PARTS)
-        for condition, copy in w_routes(b, c):
-            pl.when(condition)(copy.wait_send)
-
-    def side_sent(b):
-        passes = inside | (z == other_z0 + b) | (border & (b == side_block(1)))
-        for condition, copy in side_routes(b):
-            pl.when(condition & passes)(copy.wait_send)
+    def all_sent(sem, size):
+        at = pl.ds(0, size // (2 * key_cols))
+        remote(pf.at[at], pf.at[at], sem, sem, peer).wait_send()
+
+    part_size, chunk_size = w_rows * key_cols, g_rows * key_cols
+    counts = ((far_end, 1), (border, 2 * W_MAIN + 2), (entry, 2 * W_MAIN + W_PARTS + 4), (inside & jnp.logical_not(entry), W_PARTS + 2))
+    for kind, parts in counts:
+
+        @pl.when(carries & kind)
+        def _():
+            all_sent(sent, parts * part_size)
 
     @pl.when(carries)
     def _():
-        each(w_steps, w_sent)
-        each(blocks, side_sent)
-        remote(w, w, w_dd, w_dd, peer).wait_send()
-        remote(pa, pb, p_s, p_s, peer).wait_send()
-
-    @pl.when(sums)
-    def _():
-        at = pl.ds(0, blocks * (G_PARTS - G_MAIN) * g_rows)
-        remote(pb.at[at], pa.at[at], x_s, x_s, beside).wait_send()
-
-    d1_all().wait_send()
-    d2_all().wait_send()
-    c1_all(image_rows, ci_s, ci_r).wait_send()
+        all_sent(shared, 2 * columns * key_cols)
+
     total = y[text_rows, my_cols]
-    c1_all(text_rows, ct_s, ct_r).wait_recv()
+    c1_all(text_rows, ct_r).wait_recv()
     for i in range(1, tp):
         total = total + yr[head_of(i)[0], text_rows, :].astype(f32)
     c2_all().wait_recv()
@@ -761,19 +802,14 @@
         turned = values * cosv[...] + pltpu.roll(values, HALF, 1) * sinv[...]
         keys_out[s * LENGTH : (s + 1) * LENGTH, :] = jnp.where(live(s), turned, 0.0).astype(bf16)
 
-    remote(landed, landed, g_s, g_r, peer).wait_recv()
+    remote(landed, landed, sent, g_r, peer).wait_recv()
     wgrad_out[...] = landed[...].astype(f32) * (1.0 / rows)
 
-    for condition, parts in ((inside, G_MAIN), (jnp.logical_not(inside), G_PARTS - G_MAIN)):
-
-        @pl.when(sums & condition)
-        def _():
-            ends, passed = pl.ds(0, parts * g_rows), pl.ds(0, (g_steps - parts) * g_rows)
-            remote(chain.at[ends], above.at[ends], g_s, g_s, peer).wait_send()
-            remote(chain.at[passed], above.at[passed], ch_s, ch_s, peer).wait_send()
-
-    c1_all(text_rows, ct_s, ct_r).wait_send()
-    c2_all().wait_send()
+    @pl.when(sums)
+    def _():
+        all_sent(sent, (g_steps + blocks * sides) * chunk_size)
+
+    all_sent(small, 2 * (units - 1) * capacity * cols + (tp - 1) * (both + images) * cols)
 
 
 def write_kernel(*refs):
@@ -872,10 +908,8 @@
             pltpu.VMEM((slots, cols), bf16),
             pltpu.VMEM((block, cols), bf16),
             pltpu.VMEM((blocks, block // W_PARTS, key_cols), bf16),
-            dma(9), dma(w_steps), dma(w_steps), dma(w_steps), one,
-            one, one, one, one, one, one, one, one, one, one,
-            one, dma(g_steps), dma(g_steps), dma(g_steps), one, one, one,
-            one, dma(g_steps), dma(blocks), dma(blocks), dma(blocks),
+            dma(9), dma(w_steps * W_FINE), one, one, one, one, one, one, one, one, one,
+            dma(g_steps), dma(g_steps), dma(blocks * (G_PARTS - G_MAIN)), dma(blocks * W_FINE),
         ],
         compiler_params=pltpu.CompilerParams(
             collective_id=0, has_side_effects=True, vmem_limit_bytes=44 * 1024 * 1024

time: 50.3 us -> 48.7 us (0.968)
  Pallas kernels: 49.5 us -> 47.9 us
    pallas_call x1, Pallas kernels: 47.6 us -> 46 us  [per_device(): pl.pallas_call(functools.partial(fused_kernel, groups, fsdp, tp, capacity...]
where the time goes in v4:
time: 48.7 us; the launch traced here: 48.6 us
  Pallas kernels  47.9 us (98%)
  between operations  0.64 us (1%)
    pallas_call x1, Pallas kernels, per_device(): pl.pallas_call(functools.partial(fused_kernel, groups, fsdp, tp, capacity...  46 us
    pallas_call x1, Pallas kernels, per_device(): pl.pallas_call(write_kernel, out_shape=shapes, in_specs=[vmem] * 4, out_s...  1.91 us

profile of v4, /device:TPU:0, one launch (start us, length us, event | category | flops | bytes accessed | tf_op | source)
XLA Modules:
  0.0 48.6 jit_solution(10644195581594649138)
XLA Ops:
  0.6 46.0 %fused.1 = (bf16[512,128]{1,0:T(8,128)(2,1)S(1)}, bf16[512,2048]{1,0:T(8,128)(2,1)S(1)}, bf16[256,2048]{1,0:T(8,128)(2,1)S(1)}, f32[1024,128]{1,0:T(8,128)S(1)}) custom-call(bf16[512,2048]{1,0:T(8,128)(2,1)} %text_ref.1, bf16[256,2048]{1,0:T(8,128)(2,1)} %image_ref.1, bf16[1024,512]{1,0:T(8,128)(2,1)} %weight_ref.1, f32[1,128]{1,0:T(1,128)} %bitcast.6, ...), custom_call_target="tpu_custom_call" | custom-call | tf_op jit(solution)/shard_map/fused/pallas_call | solution.py:876
  46.7 1.9 %write.1 = (bf16[512,128]{1,0:T(8,128)(2,1)}, bf16[512,2048]{1,0:T(8,128)(2,1)}, bf16[256,2048]{1,0:T(8,128)(2,1)}, f32[1024,128]{1,0:T(8,128)}) custom-call(bf16[512,128]{1,0:T(8,128)(2,1)S(1)} %get-tuple-element.8.refs_0_, bf16[512,2048]{1,0:T(8,128)(2,1)S(1)} %get-tuple-element.9.refs_1_, bf16[256,2048]{1,0:T(8,128)(2,1)S(1)} %get-tuple-element.10.refs_2_, ...), custom_call_target="tpu_custom_call" | custom-call | tf_op jit(solution)/shard_map/write/pallas_call | solution.py:919

commit v5 on v4

--- a/solution.py
+++ b/solution.py
@@ -247,12 +247,15 @@
 W_FINE = 2
 W_NEAR_OR_FAR = (0, 0, 0, 1, 0, 1, 1, 1)
 W_PART_AT = (0, 1, 2, 0, 3, 1, 3, 2)
-FAR_STEPS = (0, 2, 4, 6, 8, 10, 10, 10, 10, 10, 13, 13, 13, 13, 16)
-BORDER_STEPS = (0, 0, 0, 0, 2, 4, 6, 8, 8, 13, 13, 16, 16, 16, 16)
-ENTRY_STEPS = (0, 0, 0, 0, 0, 0, 0, 0, 0, 4, 8, 14, 16, 16, 16)
-LAST_STEPS = (0, 0, 0, 0, 2, 4, 6, 9, 11, 13, 13, 16, 16, 16, 16)
+FAR_LEAD = 4
+FAR_STEPS = (0, 3, 6, 9, 11, 11, 11, 11, 11, 14, 14, 14, 14, 16)
+BORDER_STEPS = (0, 0, 0, 0, 2, 4, 6, 8, 8, 13, 13, 16, 16, 16)
+BORDER_SPOT = 8
+ENTRY_STEPS = (0, 0, 0, 0, 0, 0, 0, 0, 0, 4, 8, 14, 16, 16)
+ENTRY_ORDER = (5, 6, 0, 1, 7, 8, 2, 3, 9, 10, 4, 11, 12, 13, 14, 15)
+LAST_STEPS = (0, 0, 0, 0, 2, 4, 6, 9, 10, 12, 14, 16, 16, 16)
 G_PARTS = 8
-G_MAIN = 5
+G_SIDES = (3, 2)
 
 
 def fused_kernel(
@@ -310,11 +313,12 @@
         return near_block(look_up(W_NEAR_OR_FAR, n)), look_up(W_PART_AT, n)
 
     def unit_of(i):
-        v = lax.rem(me + i, units)
-        return v, (v // fsdp, lax.rem(v, fsdp), t)
+        far = units - i
+        core, plane = lax.bitwise_xor(g, far % groups), lax.bitwise_xor(z, far // groups)
+        return core * fsdp + plane, (core, plane, t)
 
     def head_of(i):
-        q = lax.rem(t + i, tp)
+        q = lax.bitwise_xor(t, tp - 1 if i == 1 else i - 1)
         return q, (g, z, q)
 
     def remote(src, dst, send, recv, device):
@@ -384,9 +388,6 @@
     loads[0].wait()
     slot_ids = lax.broadcasted_iota(jnp.int32, (slots, rows), 0)
     place_t[...] = jnp.where(slot_ids == slot_ref[...], 1.0, 0.0).astype(bf16)
-    is_img[...] = lax.dot_general(
-        place_t[...], jnp.ones((slots, cols), bf16), ROWS_TO_COLS, preferred_element_type=f32
-    )
     row_ids = lax.broadcasted_iota(jnp.int32, (LENGTH, HEAD_DIM), 0)
 
     def live(s):
@@ -463,22 +464,25 @@
                 pl.when(condition & jnp.logical_not(held & inward))(copy.start)
             w_share(b, c, h).start()
 
-    @pl.when(carries & inside)
-    def _():
-        lax.fori_loop(0, W_PARTS, lambda c, carry: (w_forward(z - z0, c), carry)[1], 0)
-
-    @pl.when(carries & jnp.logical_not(inside))
-    def _():
-        side_forward(z - other_z0)
-
     early = jnp.where(inside, near_block(1), near_block(0))
 
+    is_img[...] = lax.dot_general(
+        place_t[...], jnp.ones((slots, cols), bf16), ROWS_TO_COLS, preferred_element_type=f32
+    )
     y[...] = jnp.zeros_like(y)
     for s in range(rows // LENGTH):
         span = pl.ds(s * LENGTH, LENGTH)
         for h in range(tp):
             at = pl.ds(h * cols, cols)
             back[span, at] = jnp.where(is_img[span, :] > 0.5, 0.0, rotated_back(s, at)).astype(bf16)
+    @pl.when(carries & inside)
+    def _():
+        lax.fori_loop(0, W_PARTS, lambda c, carry: (w_forward(z - z0, c), carry)[1], 0)
+
+    @pl.when(carries & jnp.logical_not(inside))
+    def _():
+        side_forward(z - other_z0)
+
     loads[5].wait()
     image_units = lax.broadcasted_iota(jnp.int32, (units, images), 0)
     marks = jnp.where(image_units == owner_ref[...], 1.0, 0.0)
@@ -551,7 +555,7 @@
         return pl.ds(pl.multiple_of(b * block + c * g_rows, g_rows), g_rows)
 
     def x_copy(b, c):
-        i, at = b * (G_PARTS - G_MAIN) + c - G_MAIN, g_slice(b, c)
+        i, at = b * G_SIDES[0] + c - (G_PARTS - G_SIDES[0]), g_slice(b, c)
         return remote(pb.at[at], pa.at[at], sent, x_r.at[i], beside)
 
     def x_send(b, c):
@@ -608,17 +612,28 @@
             for h in range(W_FINE):
                 w_load(b, c, h).wait()
 
-        at = w_slice(b, c)
-        for which, recv in ((image_rows, ci_r), (text_rows, ct_r)):
-            y[which, :] += jnp.dot(x[which, at], w[at, :], preferred_element_type=f32)
-
-            @pl.when(n == w_steps - 1)
-            def _():
-                c1_send(which, recv)
-
-        last, kept = n == w_steps - 1, w_steps - 3
-        start = jnp.where(last, kept, n)
-        lax.fori_loop(start, jnp.where((n < kept) | last, n + 1, n), grad_step, 0)
+        last = n == w_steps - 1
+        project(n, image_rows)
+
+        @pl.when(last)
+        def _():
+            c1_send(image_rows, ci_r)
+
+        def text_step(k, carry):
+            project(k, text_rows)
+            return carry
+
+        lax.fori_loop(jnp.where(last, n - 1, n), jnp.where(n == w_steps - 2, n, n + 1), text_step, 0)
+        kept = w_steps - 3
+        lax.fori_loop(jnp.where(last, kept, n), jnp.where((n < kept) | last, n + 1, n), grad_step, 0)
+
+        @pl.when(last)
+        def _():
+            c1_send(text_rows, ct_r)
+
+    def project(n, which):
+        at = w_slice(*w_part(n))
+        y[which, :] += jnp.dot(x[which, at], w[at, :], preferred_element_type=f32)
 
     def grad_step(n, carry):
         at = w_slice(*w_part(n))
@@ -660,31 +675,33 @@
             c2(i).start()
         c2_dst[slot_rows(me), :] = c2_src[slot_rows(me), :]
 
-    def home(b, c):
-        return jnp.where(c < G_MAIN, z0, other_z0) + b
-
-    def chain_copies(b, c):
-        i, at = b * G_PARTS + c, g_slice(b, c)
+    def chain_copies(i, at, zb):
         return (
-            (z > home(b, c), remote(chain.at[at], above.at[at], sent, chain_r.at[i], (g, z - 1, t))),
-            (z < home(b, c), remote(chain.at[at], below.at[at], sent, chain_r.at[i], (g, z + 1, t))),
+            (z > zb, remote(chain.at[at], above.at[at], sent, chain_r.at[i], (g, z - 1, t))),
+            (z < zb, remote(chain.at[at], below.at[at], sent, chain_r.at[i], (g, z + 1, t))),
         )
 
     def landing(c):
         return landed.at[pl.ds(pl.multiple_of(c * g_rows, g_rows), g_rows)]
 
-    def result_copy(b, c, q):
-        return remote(
-            chain.at[g_slice(b, c), q * cols : (q + 1) * cols], landing(c), sent, g_r, (1 - g, z, q)
-        )
+    def result_copy(at, c, q):
+        return remote(chain.at[at, q * cols : (q + 1) * cols], landing(c), sent, g_r, (1 - g, z, q))
 
     def g_step(m):
-        own = jnp.where(inside, m >= blocks * (G_PARTS - G_MAIN), m < blocks * G_MAIN)
-        own_m = jnp.where(inside, m - blocks * (G_PARTS - G_MAIN), m)
-        other_m = jnp.where(inside, m, m - blocks * G_MAIN)
-        b = jnp.where(own, near_block(blocks - 1 - own_m // G_MAIN), far_other(other_m // (G_PARTS - G_MAIN)))
-        c = jnp.where(own, lax.rem(own_m, G_MAIN), G_MAIN + lax.rem(other_m, G_PARTS - G_MAIN))
-        i, at, zb = b * G_PARTS + c, g_slice(b, c), home(b, c)
+        own = jnp.where(inside, m >= all_sides, m < g_steps - all_sides)
+        own_m = jnp.where(inside, m - all_sides, m)
+        other_m = jnp.where(inside, m, m - (g_steps - all_sides))
+        first_own = G_PARTS - jnp.where(inside & jnp.logical_not(entry), G_SIDES[0], G_SIDES[1])
+        first_other = jnp.where(far_end, G_SIDES[0], G_SIDES[1])
+        own_k, other_k = jnp.where(own_m >= first_own, 1, 0), jnp.where(other_m >= first_other, 1, 0)
+        own_c = own_m - own_k * first_own
+        other_c = G_PARTS + jnp.where(other_k == 1, other_m - all_sides, other_m - first_other)
+        b = jnp.where(own, near_block(blocks - 1 - own_k), far_other(other_k))
+        c = jnp.where(own, own_c, other_c)
+        zb = jnp.where(own, z0, other_z0) + b
+        slot_b = jnp.where(own, b, blocks - 1 - b)
+        i, at = slot_b * G_PARTS + c, g_slice(slot_b, c)
+        came_at = g_slice(b, c)
 
         @pl.when(own)
         def _():
@@ -694,7 +711,7 @@
         @pl.when(jnp.logical_not(own))
         def _():
             x_copy(b, c).wait_recv()
-            pf[at, :] = pa[at, :].astype(f32)
+            pf[at, :] = pa[came_at, :].astype(f32)
 
         from_above, from_below = (z >= zb) & (z < fsdp - 1), (z <= zb) & (z > 0)
         pair = pl.ds(0, 2 * g_rows)
@@ -714,31 +731,31 @@
                 pf[at, :] += source[at, :].astype(f32)
 
         chain[at, :] = pf[at, :].astype(bf16)
-        for condition, copy in chain_copies(b, c):
+        for condition, copy in chain_copies(i, at, zb):
             pl.when(condition)(copy.start)
 
         @pl.when(z == zb)
         def _():
             for q in range(tp):
-                result_copy(b, c, q).start()
+                result_copy(at, c, q).start()
 
     ratio = g_steps // w_steps
     half = w_steps // 2
-    mains, sides = blocks * G_MAIN, G_PARTS - G_MAIN
-    lead = mains // ratio
+    all_sides = sum(G_SIDES)
+    mains = g_steps - all_sides
+    lead = FAR_LEAD
     turns = len(FAR_STEPS) - 1
     sums = jnp.logical_not(carries)
     late = sums & far_end
     w_at = jnp.where(late, lead, 0)
     c2_at = jnp.where(far_end, lead + w_steps - 1, jnp.where(entry, w_steps + 2, w_steps + 1))
     c2_at = jnp.where(carries, w_steps - 1, c2_at)
-    spot = mains - ratio
+    spot = BORDER_SPOT
 
     def in_turn(m):
+        sides = G_SIDES[1]
         moved = jnp.where(m < spot + sides, m - spot + mains, jnp.where(m < mains + sides, m - sides, m))
-        group, place = m // (2 * ratio), lax.rem(m, 2 * ratio)
-        woven = jnp.where(place < ratio, blocks * sides, -ratio) + group * ratio + place
-        woven = jnp.where(m < 2 * blocks * sides, woven, m)
+        woven = look_up(ENTRY_ORDER, m)
         return jnp.where(border & (m >= spot), moved, jnp.where(entry, woven, m))
 
     def turn(s, carry):
@@ -760,7 +777,10 @@
 
         @pl.when(sums & (x_at >= 0))
         def _():
-            lax.fori_loop(G_MAIN, G_PARTS, lambda c, unused: (x_send(near_block(blocks - 1 - x_at), c), unused)[1], 0)
+            b = near_block(blocks - 1 - x_at)
+            of_entry = b == jnp.where(upward, 0, blocks - 1)
+            start = G_PARTS - jnp.where(of_entry, G_SIDES[0], G_SIDES[1])
+            lax.fori_loop(start, G_PARTS, lambda c, unused: (x_send(b, c), unused)[1], 0)
 
         @pl.when((n >= 0) & (n < w_steps))
         def _():
@@ -807,7 +827,7 @@
 
     @pl.when(sums)
     def _():
-        all_sent(sent, (g_steps + blocks * sides) * chunk_size)
+        all_sent(sent, (g_steps + all_sides) * chunk_size)
 
     all_sent(small, 2 * (units - 1) * capacity * cols + (tp - 1) * (both + images) * cols)
 
@@ -833,7 +853,7 @@
 
 def fits(groups, fsdp, tp, rows, head_cols, block):
     units = groups * fsdp
-    if groups != 2 or units % tp or head_cols != HEAD_DIM or rows % LENGTH:
+    if groups != 2 or units % tp or units & (units - 1) or tp & (tp - 1) or head_cols != HEAD_DIM or rows % LENGTH:
         return False
     blocks = units // tp
     return blocks == 2 and fsdp == 2 * blocks and tp % 2 == 0 and block % (G_PARTS * HEAD_DIM) == 0 and (rows // units) % 16 == 0
@@ -909,7 +929,7 @@
             pltpu.VMEM((block, cols), bf16),
             pltpu.VMEM((blocks, block // W_PARTS, key_cols), bf16),
             dma(9), dma(w_steps * W_FINE), one, one, one, one, one, one, one, one, one,
-            dma(g_steps), dma(g_steps), dma(blocks * (G_PARTS - G_MAIN)), dma(blocks * W_FINE),
+            dma(g_steps), dma(g_steps), dma(blocks * G_SIDES[0]), dma(blocks * W_FINE),
         ],
         compiler_params=pltpu.CompilerParams(
             collective_id=0, has_side_effects=True, vmem_limit_bytes=44 * 1024 * 1024

time: 48.7 us -> 48.1 us (0.988)
  Pallas kernels: 47.9 us -> 47.2 us
    pallas_call x1, Pallas kernels: 46 us -> 45.3 us  [per_device(): pl.pallas_call(functools.partial(fused_kernel, groups, fsdp, tp, capacity...]
where the time goes in v5:
time: 48.1 us; the launch traced here: 47.9 us
  Pallas kernels  47.2 us (98%)
  between operations  0.64 us (1%)
    pallas_call x1, Pallas kernels, per_device(): pl.pallas_call(functools.partial(fused_kernel, groups, fsdp, tp, capacity...  45.3 us
    pallas_call x1, Pallas kernels, per_device(): pl.pallas_call(write_kernel, out_shape=shapes, in_specs=[vmem] * 4, out_s...  1.91 us

profile of v5, /device:TPU:0, one launch (start us, length us, event | category | flops | bytes accessed | tf_op | source)
XLA Modules:
  0.0 47.9 jit_solution(10644929678608098860)
XLA Ops:
  0.6 45.3 %fused.1 = (bf16[512,128]{1,0:T(8,128)(2,1)S(1)}, bf16[512,2048]{1,0:T(8,128)(2,1)S(1)}, bf16[256,2048]{1,0:T(8,128)(2,1)S(1)}, f32[1024,128]{1,0:T(8,128)S(1)}) custom-call(bf16[512,2048]{1,0:T(8,128)(2,1)} %text_ref.1, bf16[256,2048]{1,0:T(8,128)(2,1)} %image_ref.1, bf16[1024,512]{1,0:T(8,128)(2,1)} %weight_ref.1, f32[1,128]{1,0:T(1,128)} %bitcast.6, ...), custom_call_target="tpu_custom_call" | custom-call | tf_op jit(solution)/shard_map/fused/pallas_call | solution.py:896
  46.0 1.9 %write.1 = (bf16[512,128]{1,0:T(8,128)(2,1)}, bf16[512,2048]{1,0:T(8,128)(2,1)}, bf16[256,2048]{1,0:T(8,128)(2,1)}, f32[1024,128]{1,0:T(8,128)}) custom-call(bf16[512,128]{1,0:T(8,128)(2,1)S(1)} %get-tuple-element.8.refs_0_, bf16[512,2048]{1,0:T(8,128)(2,1)S(1)} %get-tuple-element.9.refs_1_, bf16[256,2048]{1,0:T(8,128)(2,1)S(1)} %get-tuple-element.10.refs_2_, ...), custom_call_target="tpu_custom_call" | custom-call | tf_op jit(solution)/shard_map/write/pallas_call | solution.py:939

commit v6 on v5

--- a/solution.py
+++ b/solution.py
@@ -250,7 +250,7 @@
 FAR_LEAD = 4
 FAR_STEPS = (0, 3, 6, 9, 11, 11, 11, 11, 11, 14, 14, 14, 14, 16)
 BORDER_STEPS = (0, 0, 0, 0, 2, 4, 6, 8, 8, 13, 13, 16, 16, 16)
-BORDER_SPOT = 8
+BORDER_SPOT = 11
 ENTRY_STEPS = (0, 0, 0, 0, 0, 0, 0, 0, 0, 4, 8, 14, 16, 16)
 ENTRY_ORDER = (5, 6, 0, 1, 7, 8, 2, 3, 9, 10, 4, 11, 12, 13, 14, 15)
 LAST_STEPS = (0, 0, 0, 0, 2, 4, 6, 9, 10, 12, 14, 16, 16, 16)
@@ -624,12 +624,13 @@
             return carry
 
         lax.fori_loop(jnp.where(last, n - 1, n), jnp.where(n == w_steps - 2, n, n + 1), text_step, 0)
+
+        @pl.when(last)
+        def _():
+            c1_send(text_rows, ct_r)
+
         kept = w_steps - 3
         lax.fori_loop(jnp.where(last, kept, n), jnp.where((n < kept) | last, n + 1, n), grad_step, 0)
-
-        @pl.when(last)
-        def _():
-            c1_send(text_rows, ct_r)
 
     def project(n, which):
         at = w_slice(*w_part(n))

time: 48.1 us -> 48.1 us (level)
  no operation moved by 1% of the time
where the time goes in v6:
time: 48.1 us; the launch traced here: 47.9 us
  Pallas kernels  47.2 us (98%)
  between operations  0.64 us (1%)
    pallas_call x1, Pallas kernels, per_device(): pl.pallas_call(functools.partial(fused_kernel, groups, fsdp, tp, capacity...  45.3 us
    pallas_call x1, Pallas kernels, per_device(): pl.pallas_call(write_kernel, out_shape=shapes, in_specs=[vmem] * 4, out_s...  1.91 us

profile of v6, /device:TPU:0, one launch (start us, length us, event | category | flops | bytes accessed | tf_op | source)
XLA Modules:
  0.0 47.9 jit_solution(15284401359974304399)
XLA Ops:
  0.6 45.3 %fused.1 = (bf16[512,128]{1,0:T(8,128)(2,1)S(1)}, bf16[512,2048]{1,0:T(8,128)(2,1)S(1)}, bf16[256,2048]{1,0:T(8,128)(2,1)S(1)}, f32[1024,128]{1,0:T(8,128)S(1)}) custom-call(bf16[512,2048]{1,0:T(8,128)(2,1)} %text_ref.1, bf16[256,2048]{1,0:T(8,128)(2,1)} %image_ref.1, bf16[1024,512]{1,0:T(8,128)(2,1)} %weight_ref.1, f32[1,128]{1,0:T(1,128)} %bitcast.6, ...), custom_call_target="tpu_custom_call" | custom-call | tf_op jit(solution)/shard_map/fused/pallas_call | solution.py:897
  46.0 1.9 %write.1 = (bf16[512,128]{1,0:T(8,128)(2,1)}, bf16[512,2048]{1,0:T(8,128)(2,1)}, bf16[256,2048]{1,0:T(8,128)(2,1)}, f32[1024,128]{1,0:T(8,128)}) custom-call(bf16[512,128]{1,0:T(8,128)(2,1)S(1)} %get-tuple-element.8.refs_0_, bf16[512,2048]{1,0:T(8,128)(2,1)S(1)} %get-tuple-element.9.refs_1_, bf16[256,2048]{1,0:T(8,128)(2,1)S(1)} %get-tuple-element.10.refs_2_, ...), custom_call_target="tpu_custom_call" | custom-call | tf_op jit(solution)/shard_map/write/pallas_call | solution.py:940
